TPU v7x, 32 devices: a 4x4x1 block of a 4x4x8 slice. The times are simulated.
32 devices in a mesh: dp: 1 (over z), col: 4 (over y), row: 8 (over x, core).
Axes of the slice: x: 4, y: 4, z: 1, core: 2. Of those that a mesh axis runs over, the one named last changes fastest.
The devices are a block of a 4x4x8 slice.
Arguments:
- seq_in: bfloat16 [64, 16, 2048], P(None, 'dp', 'row')
- w_in1: bfloat16 [2048, 8192], P('row', 'col')
- w_rec1: bfloat16 [2048, 8192], P('row', 'col')
- b_gate1: float32 [8192], P(('col', 'row'))
- w_in2: bfloat16 [2048, 8192], P('row', 'col')
- w_rec2: bfloat16 [2048, 8192], P('row', 'col')
- b_gate2: float32 [8192], P(('col', 'row'))
- h_init: float32 [2, 16, 2048], P(None, 'dp', 'row')
- c_init: float32 [2, 16, 2048], P(None, 'dp', 'row')
Outputs:
- output 1: bfloat16 [64, 16, 2048], P(None, 'dp', ('row', 'col'))
- output 2: float32 [16, 2048], P('dp', ('row', 'col'))
- output 3: float32 [16, 2048], P('dp', ('row', 'col'))
All inputs are finite; a program needn't handle non-finite values.
Results may differ from a plain program's by a relative error of at most 0.00347769.
Values are sent between devices in bfloat16 or wider.
A program may use at most 768 MiB of HBM per device.

v0:
```python
import jax
import jax.numpy as jnp
from jax import lax
from jax.sharding import PartitionSpec as P


def gate_update(z_own, c_prev):
    unit_dev = c_prev.shape[-1]
    in_gate = jax.nn.sigmoid(z_own[:, :unit_dev])
    forget = jax.nn.sigmoid(z_own[:, unit_dev:2 * unit_dev])
    cell_in = jnp.tanh(z_own[:, 2 * unit_dev:3 * unit_dev])
    out_gate = jax.nn.sigmoid(z_own[:, 3 * unit_dev:])
    c_new = forget * c_prev + in_gate * cell_in
    h_new = (out_gate * jnp.tanh(c_new)).astype(jnp.bfloat16)
    return h_new, c_new


def solution(mesh):
    def lstm_layer(in_rows, w_in, w_rec, b_own, h_rows, c_own, keep_rows):
        def lstm_step(carry_in, in_step):
            h_prev, c_prev = carry_in
            part_sum = jnp.dot(in_step, w_in, preferred_element_type=jnp.float32)
            part_sum = part_sum + jnp.dot(h_prev, w_rec, preferred_element_type=jnp.float32)
            z_own = lax.psum_scatter(part_sum, "row", scatter_dimension=1, tiled=True) + b_own
            h_own, c_new = gate_update(z_own, c_prev)
            h_next = lax.all_gather(h_own, "col", axis=1, tiled=True)
            return (h_next, c_new), (h_next if keep_rows else h_own)

        return lax.scan(lstm_step, (h_rows, c_own), in_rows)

    def local_program(seq_in, w_in1, w_rec1, b_gate1, w_in2, w_rec2, b_gate2, h_init, c_init):
        unit_dev = b_gate1.shape[0] // 4
        col_index = lax.axis_index("col")

        def own_cells(layer_idx):
            return lax.dynamic_slice_in_dim(c_init[layer_idx], col_index * unit_dev, unit_dev, axis=1)

        carry_one, h1_rows = lstm_layer(seq_in, w_in1, w_rec1, b_gate1, h_init[0].astype(jnp.bfloat16), own_cells(0), True)
        carry_two, h2_own = lstm_layer(h1_rows, w_in2, w_rec2, b_gate2, h_init[1].astype(jnp.bfloat16), own_cells(1), False)
        return h2_own, carry_one[1], carry_two[1]

    row_spec = P(None, "dp", "row")
    weight_spec = P("row", "col")
    bias_spec = P(("col", "row"))
    seq_out_spec = P(None, "dp", ("row", "col"))
    cell_out_spec = P("dp", ("row", "col"))
    return jax.shard_map(
        local_program,
        mesh=mesh,
        in_specs=(row_spec, weight_spec, weight_spec, bias_spec, weight_spec, weight_spec, bias_spec, row_spec, row_spec),
        out_specs=(seq_out_spec, cell_out_spec, cell_out_spec),
        check_vma=False,
    )
```

profile of v0, /device:TPU:97, one launch (start us, length us, event | category | flops | bytes accessed | tf_op | source)
XLA Modules:
  0.0 5526.3 jit_solution(4705853495786674996)
XLA Ops:
  9.4 2755.3 %while.28 = (s32[]{:T(128)}, bf16[16,256]{1,0:T(8,128)(2,1)S(1)}, f32[16,64]{1,0:T(8,128)S(1)}, bf16[64,16,256]{2,1,0:T(8,128)(2,1)S(1)}, bf16[64,16,256]{2,1,0:...) while((s32[]{:T(128)}, bf16[16,256]{1,0:T(8,128)(2,1)S(1)}, ...), condition=%wide.region_2.3_spmd, body=%wide.region_0.2_spmd.sunk | while | flops 33605632 | bytes 7263409 | solution.py:29
  11.9 30.4 reduce-scatter.3.cloned.1.call-done
  55.6 30.0 reduce-scatter.3.cloned.1.call-done
  270.7 30.0 reduce-scatter.3.cloned.1.call-done
  313.8 30.0 reduce-scatter.3.cloned.1.call-done
  443.1 30.0 reduce-scatter.3.cloned.1.call-done
  529.2 30.0 reduce-scatter.3.cloned.1.call-done
  872.9 30.1 reduce-scatter.3.cloned.1.call-done
  916.1 30.0 reduce-scatter.3.cloned.1.call-done
  959.3 30.0 reduce-scatter.3.cloned.1.call-done
  1045.3 30.1 reduce-scatter.3.cloned.1.call-done
  1174.3 30.0 reduce-scatter.3.cloned.1.call-done
  1217.5 30.1 reduce-scatter.3.cloned.1.call-done
  1303.6 30.0 reduce-scatter.3.cloned.1.call-done
  1476.0 30.0 reduce-scatter.3.cloned.1.call-done
  1734.3 30.0 reduce-scatter.3.cloned.1.call-done
  1777.5 30.0 reduce-scatter.3.cloned.1.call-done
  2121.3 30.0 reduce-scatter.3.cloned.1.call-done
  2207.3 30.0 reduce-scatter.3.cloned.1.call-done
  2293.3 30.1 reduce-scatter.3.cloned.1.call-done
  2379.8 30.0 reduce-scatter.3.cloned.1.call-done
  2551.9 30.0 reduce-scatter.3.cloned.1.call-done
  2638.3 30.1 reduce-scatter.3.cloned.1.call-done
  2765.4 2753.5 %while.29 = (s32[]{:T(128)}, bf16[16,256]{1,0:T(8,128)(2,1)S(1)}, f32[16,64]{1,0:T(8,128)S(1)}, bf16[64,16,64]{2,1,0:T(8,128)(2,1)}, bf16[64,16,256]{2,1,0:T(8,1...) while((s32[]{:T(128)}, bf16[16,256]{1,0:T(8,128)(2,1)S(1)}, ...), condition=%wide.region_5.6_spmd, body=%wide.region_3.5_spmd.sunk | while | flops 33605632 | bytes 7251121 | solution.py:29
  (1594 shorter events, 4847.7 us)
Async XLA Ops:
  9.4 33.0 reduce-scatter.3.cloned.1.call-start
  53.0 32.6 reduce-scatter.3.cloned.1.call-start
  268.1 32.6 reduce-scatter.3.cloned.1.call-start
  311.2 32.7 reduce-scatter.3.cloned.1.call-start
  440.5 32.6 reduce-scatter.3.cloned.1.call-start
  526.6 32.6 reduce-scatter.3.cloned.1.call-start
  784.2 32.6 reduce-scatter.3.cloned.1.call-start
  870.2 32.7 reduce-scatter.3.cloned.1.call-start
  913.5 32.6 reduce-scatter.3.cloned.1.call-start
  956.7 32.6 reduce-scatter.3.cloned.1.call-start
  1042.7 32.7 reduce-scatter.3.cloned.1.call-start
  1171.7 32.6 reduce-scatter.3.cloned.1.call-start
  1214.9 32.7 reduce-scatter.3.cloned.1.call-start
  1301.0 32.6 reduce-scatter.3.cloned.1.call-start
  1473.4 32.7 reduce-scatter.3.cloned.1.call-start
  1602.4 32.6 reduce-scatter.3.cloned.1.call-start
  1731.7 32.7 reduce-scatter.3.cloned.1.call-start
  1774.9 32.6 reduce-scatter.3.cloned.1.call-start
  2118.6 32.7 reduce-scatter.3.cloned.1.call-start
  2204.7 32.6 reduce-scatter.3.cloned.1.call-start
  2290.7 32.7 reduce-scatter.3.cloned.1.call-start
  2377.2 32.7 reduce-scatter.3.cloned.1.call-start
  2549.3 32.6 reduce-scatter.3.cloned.1.call-start
  2635.7 32.7 reduce-scatter.3.cloned.1.call-start
  (237 other events, 3547.2 us)
Sparse Core Ops, SparseCore 0:
  13.0 29.3 reduce-scatter.2
  314.9 28.9 reduce-scatter.2
  873.9 28.9 reduce-scatter.2
  1046.4 28.9 reduce-scatter.2
  1218.5 28.9 reduce-scatter.2
  1390.7 28.9 reduce-scatter.2
  1562.8 28.9 reduce-scatter.2
  1907.5 28.9 reduce-scatter.2
  2079.0 28.9 reduce-scatter.2
  2294.4 29.0 reduce-scatter.2
  2466.9 29.0 reduce-scatter.2
  2639.3 28.9 reduce-scatter.2
  2811.3 28.9 reduce-scatter.4
  3155.1 28.9 reduce-scatter.4
  3370.7 28.9 reduce-scatter.4
  3543.1 28.9 reduce-scatter.4
  3714.8 28.9 reduce-scatter.4
  3887.2 28.9 reduce-scatter.4
  4403.1 28.9 reduce-scatter.4
  4574.9 29.0 reduce-scatter.4
  4747.3 29.0 reduce-scatter.4
  4962.8 28.9 reduce-scatter.4
  5177.4 28.9 reduce-scatter.4
  5349.5 28.9 reduce-scatter.4
  (104 shorter events, 2999.5 us)
where the time goes:
time: 5540 us; the launch traced here: 5530 us
  waiting for transfers between devices  3790 us (68%)
  blocking collectives  1230 us (22%)
  matrix products  317 us (6%)
  other arithmetic  142 us (3%)
    reduce_scatter x128, waiting for transfers between devices, lstm_step(): lax.psum_scatter(part_sum, 'row', scatter_dimension=1, tiled=True) + b_own  3780 us
    all_gather x128, blocking collectives, lstm_step(): h_next = lax.all_gather(h_own, 'col', axis=1, tiled=True)  1230 us
    dot_general x128, matrix products, lstm_step(): part_sum = jnp.dot(in_step, w_in, preferred_element_type=jnp.float32)  200 us
    dot_general x128, matrix products, lstm_step(): jnp.dot(h_prev, w_rec, preferred_element_type=jnp.float32)  117 us
  transfers between devices with their start and end apart: 128, of which 128 were waited for; matrix products, arithmetic and copies ran while one was open for 0% of the time, Pallas kernels for 0%

commit v1 on v0

v1 whole, which is shorter than its diff:
```python
import functools

import jax
import jax.numpy as jnp
from jax import lax
from jax.experimental import pallas as pl
from jax.experimental.pallas import tpu as pltpu
from jax.sharding import PartitionSpec as P

MESH = pl.DeviceIdType.MESH
F32, BF16 = jnp.float32, jnp.bfloat16
AHEAD = 4
OUT_STEPS = 8


def sigmoid(v):
    return 0.5 * jnp.tanh(0.5 * v) + 0.5


def lstm_kernel(
    n_row, n_col, wr1, wr2, wi1, wi2, x_in, bias, h0, c0, h2_out, c1_out, c2_out,
    wbuf, wi1b, wi2b, xb, bb, bias2, hist, za, zb, h1in, zout, zpre, cst, hin, cin,
    w_send, w_recv, w_relay, rel_recv, rel_send, in_send, in_recv, in_local, hc_send, hin_recv, cin_recv,
    hx_send, hx_recv, za_recv, zb_recv, z_send, h1_send, h1_recv, o_send, o_recv, c_send, c_recv,
):
    steps = x_in.shape[0]
    n_x = n_row // 2
    n_out = steps // OUT_STEPS
    col, row = lax.axis_index("col"), lax.axis_index("row")
    xx, cc = row // 2, row % 2
    head_chip = xx % 2 == 0
    layer = xx // 2
    is_rec = head_chip & (cc == 1)
    is_relay = jnp.logical_not(head_chip) & (cc == 0)
    is_input = jnp.logical_not(is_rec) & jnp.logical_not(is_relay)

    def at(x, c):
        return {"row": x * 2 + c}

    def remote(src, dst, ssem, rsem, dev):
        return pltpu.make_async_remote_copy(
            src_ref=src, dst_ref=dst, send_sem=ssem, recv_sem=rsem, device_id=dev, device_id_type=MESH)

    barrier = pltpu.get_barrier_semaphore()
    for d in range(1, n_row):
        pl.semaphore_signal(barrier, inc=1, device_id={"row": (row + d) % n_row}, device_id_type=MESH)
    for d in range(1, n_col):
        pl.semaphore_signal(barrier, inc=1, device_id={"col": (col + d) % n_col}, device_id_type=MESH)
    pl.semaphore_wait(barrier, n_row + n_col - 2)

    def weight_copies(l, go):
        wr = (wr1, wr2)[l]
        hx = 2 * l
        at_head = (xx == hx) & (cc == 1)
        relayed = ((xx - hx + n_x) % n_x == 2) & (cc == 0)
        own = pltpu.make_async_copy(wr, wbuf.at[:, row], w_send.at[l])
        direct = remote(wr, wbuf.at[:, row], w_send.at[l], w_recv.at[row], at(hx, 1))
        parts = [
            remote(wr.at[j], wbuf.at[j, row], rel_send.at[j], rel_recv.at[j], at((hx + 1) % n_x, 0))
            for j in range(n_col)
        ]

        @pl.when(at_head)
        def _():
            own.start() if go else own.wait()

        @pl.when(relayed)
        def _():
            for part in parts:
                part.start() if go else part.wait_send()

        @pl.when(jnp.logical_not(at_head) & jnp.logical_not(relayed))
        def _():
            direct.start() if go else direct.wait_send()

    def small_copies(l, go):
        hx = 2 * l
        at_head = (xx == hx) & (cc == 1)
        own = [
            pltpu.make_async_copy(h0.at[l], hin.at[row], hc_send.at[l, 0]),
            pltpu.make_async_copy(c0.at[l], cin.at[row], hc_send.at[l, 1]),
        ]
        away = [
            remote(h0.at[l], hin.at[row], hc_send.at[l, 0], hin_recv.at[row], at(hx, 1)),
            remote(c0.at[l], cin.at[row], hc_send.at[l, 1], cin_recv.at[row], at(hx, 1)),
        ]

        @pl.when(at_head)
        def _():
            for cp in own:
                cp.start() if go else cp.wait()

        @pl.when(jnp.logical_not(at_head))
        def _():
            for cp in away:
                cp.start() if go else cp.wait_send()

    pairs = [(x_in, xb.at[cc]), (wi1, wi1b.at[cc]), (bias, bb.at[cc]), (wi2, wi2b.at[:, cc])]
    to_input = [remote(s, d, in_send.at[i], in_recv.at[i], at(xx, 1 - cc)) for i, (s, d) in enumerate(pairs)]
    to_self = [pltpu.make_async_copy(s, d, in_local.at[i]) for i, (s, d) in enumerate(pairs)]
    others = [xb.at[1 - cc], wi1b.at[1 - cc], bb.at[1 - cc], wi2b.at[:, 1 - cc]]
    from_other = [remote(s, d, in_send.at[i], in_recv.at[i], at(xx, 1 - cc))
                  for i, ((s, _), d) in enumerate(zip(pairs, others))]

    @pl.when(is_input)
    def _():
        for cp in to_self:
            cp.start()

    @pl.when(jnp.logical_not(is_input))
    def _():
        for cp in to_input:
            cp.start()

    for l in range(2):
        small_copies(l, True)
    for l in range(2):
        weight_copies(l, True)

    @pl.when(is_relay)
    def _():
        origin = ((xx + 1) % n_x) * 2
        dst = at((xx + n_x - 1) % n_x, 1)
        for j in range(n_col):
            remote(wr1.at[j], wbuf.at[j, origin], rel_send.at[j], rel_recv.at[j], dst).wait_recv()
            remote(wbuf.at[j, origin], wbuf.at[j, origin], rel_send.at[j], w_relay.at[j], dst).start()
        for j in range(n_col):
            remote(wbuf.at[j, origin], wbuf.at[j, origin], rel_send.at[j], w_relay.at[j], dst).wait_send()

    @pl.when(is_rec)
    def _():
        last = (col + 2) % n_col

        def peer(d):
            return {"col": (col + d) % n_col}

        def h_copy(t, owner, half, d, par):
            ref = hist.at[t, owner, half]
            return remote(ref, ref, hx_send.at[par, d - 1, half], hx_recv.at[par, owner, half], peer(d))

        def w_half(owner, half):
            return wbuf.at[owner, pl.ds(half * 4, 4)]

        def product(t, owner, half):
            w = wbuf[owner, half * 4:half * 4 + 4].reshape(256, 2048)
            return jnp.dot(hist[t, owner, half], w, preferred_element_type=F32)

        def z_arrival(t):
            return remote(za.at[t], za.at[t], z_send.at[0, 0], za_recv.at[t], at(xx, 0))

        def forward(t, go):
            for x in range(n_x):
                src = hist.at[t + 1, :, x // 2, :, pl.ds((x % 2) * 128, 128)]
                cp = remote(src, h1in.at[t], h1_send.at[x], h1_recv.at[t], at(x, x % 2))
                cp.start() if go else cp.wait_send()

        def out_copies(n, go):
            rows = pl.ds(n * OUT_STEPS, OUT_STEPS)
            for r in range(n_row):
                x = r // 2
                src = hist.at[pl.ds(n * OUT_STEPS + 1, OUT_STEPS), col, x // 2, :, pl.ds((x % 2) * 128, 128)]
                own = pltpu.make_async_copy(src, h2_out.at[rows], o_send.at[r])
                away = remote(src, h2_out.at[rows], o_send.at[r], o_recv.at[n], {"row": r})
                if r == 5:
                    own.start() if go else own.wait()
                else:
                    away.start() if go else away.wait_send()

        for r in range(n_row):
            @pl.when(row != r)
            def _(r=r):
                remote(h0.at[0], hin.at[r], hc_send.at[0, 0], hin_recv.at[r], at(xx, 0)).wait_recv()
                remote(c0.at[0], cin.at[r], hc_send.at[0, 1], cin_recv.at[r], at(xx, 0)).wait_recv()
        for l in range(2):
            @pl.when(layer == l)
            def _(l=l):
                small_copies(l, False)
        for x in range(n_x):
            cst[x // 2, :, (x % 2) * 128:(x % 2) * 128 + 128] = cin[2 * x] + cin[2 * x + 1]
        hist[0, last] = jnp.zeros(hist.shape[2:], BF16)
        for l in range(2):
            @pl.when(layer == l)
            def _(l=l):
                weight_copies(l, False)
        relayed = ((xx + 2) % n_x) * 2
        for r in range(n_row):
            @pl.when((row != r) & (relayed != r))
            def _(r=r):
                remote(wr1, wbuf.at[:, r], w_send.at[0], w_recv.at[r], at(xx, 0)).wait_recv()
        for j in range(n_col):
            remote(wbuf.at[j, relayed], wbuf.at[j, relayed], rel_send.at[j], w_relay.at[j], at(xx, 0)).wait_recv()

        z_arrival(0).wait_recv()
        zpre[...] = za[0]
        for r in range(n_row):
            w = wbuf[:, r].reshape(256, 2048)
            zpre[...] += jnp.dot(hin[r], w, preferred_element_type=F32)

        def step(t, carry):
            par, par_before = t % 2, (t + 1) % 2
            exchange = (t < steps - 1) | (layer == 0)

            @pl.when(t > 0)
            def _():
                h_copy(t, last, 0, 2, par_before).wait_recv()

            zpre[...] += product(t, last, 0)

            @pl.when(t > 0)
            def _():
                h_copy(t, last, 1, 2, par_before).wait_recv()

            h_last = hist[t, last, 1]
            for half in range(2):
                z = []
                for m in range(4):
                    cols = slice(half * 1024 + m * 256, half * 1024 + m * 256 + 256)
                    w = wbuf[last, 4:8, :, cols].reshape(256, 256)
                    z.append(jnp.dot(h_last, w, preferred_element_type=F32) + zpre[:, cols])
                c_new = sigmoid(z[1]) * cst[half] + sigmoid(z[0]) * jnp.tanh(z[2])
                cst[half] = c_new
                hist[t + 1, col, half] = (sigmoid(z[3]) * jnp.tanh(c_new)).astype(BF16)

                @pl.when(exchange)
                def _(half=half):
                    for d in (2, 1, 3):
                        h_copy(t + 1, col, half, d, par).start()

            @pl.when((t > 0) & (layer == 0))
            def _():
                forward(t - 1, True)

            @pl.when(t < steps - 1)
            def _():
                acc = product(t + 1, col, 0) + product(t + 1, col, 1)
                z_arrival(t + 1).wait_recv()
                zpre[...] = acc + za[t + 1]
                for d in (1, 3):
                    owner = (col + d) % n_col
                    h_copy(t + 1, owner, 0, d, par).wait_recv()
                    h_copy(t + 1, owner, 1, d, par).wait_recv()
                    zpre[...] += product(t + 1, owner, 0) + product(t + 1, owner, 1)

            @pl.when((t > 0) & (layer == 0))
            def _():
                forward(t - 1, False)

            @pl.when(exchange)
            def _():
                for d in (2, 1, 3):
                    for half in range(2):
                        h_copy(t + 1, col, half, d, par).wait_send()

            @pl.when((layer == 1) & (t % OUT_STEPS == OUT_STEPS - 1))
            def _():
                n = t // OUT_STEPS

                @pl.when(n > 0)
                def _():
                    out_copies(n - 1, False)

                out_copies(n, True)

            return carry

        lax.fori_loop(0, steps, step, 0)

        def c_copies(l, go):
            for r in range(n_row):
                x = r // 2
                src = cst.at[x // 2, :, pl.ds((x % 2) * 128, 128)]
                out = (c1_out, c2_out)[l]
                if r == 4 * l + 1:
                    cp = pltpu.make_async_copy(src, out, c_send.at[r])
                    cp.start() if go else cp.wait()
                else:
                    cp = remote(src, out, c_send.at[r], c_recv.at[l], {"row": r})
                    cp.start() if go else cp.wait_send()

        @pl.when(layer == 0)
        def _():
            c_copies(0, True)
            for d in (1, 3, 2):
                for half in range(2):
                    h_copy(steps, (col + d) % n_col, half, d, (steps - 1) % 2).wait_recv()
            forward(steps - 1, True)
            forward(steps - 1, False)
            c_copies(0, False)

        @pl.when(layer == 1)
        def _():
            c_copies(1, True)
            out_copies(n_out - 1, False)
            c_copies(1, False)

    @pl.when(is_input)
    def _():
        for cp in to_self:
            cp.wait()
        for cp in from_other:
            cp.wait_recv()
        bias2[...] = bb[0] + bb[1]
        place = [xx, (xx + 2) % n_x]

        def arrival(buf, sem, u):
            return remote(buf.at[u], buf.at[u], z_send.at[0, 0], sem.at[u], at(xx, 1 - cc))

        def departure(l, u, start):
            p = place[l]
            dst_x = jnp.where(p == 0, xx, jnp.where(p == 1, (xx + n_x - 1) % n_x, (xx + 1) % n_x))
            dst_c = jnp.where(p == 0, 1, dst_x % 2)
            src = zout.at[l, u % 2]
            to_a = remote(src, za.at[u], z_send.at[l, u % 2], za_recv.at[u], at(dst_x, dst_c))
            if not start:
                to_a.wait_send()
                return
            to_b = remote(src, zb.at[u], z_send.at[l, u % 2], zb_recv.at[u], at(dst_x, dst_c))

            @pl.when(p == 3)
            def _():
                to_b.start()

            @pl.when(p != 3)
            def _():
                to_a.start()

        def input_sum(l, u):
            p = place[l]

            @pl.when(u >= 2)
            def _():
                departure(l, u - 2, False)

            if l == 0:
                part = jnp.dot(xb[0, u], wi1b[0], preferred_element_type=F32)
                part += jnp.dot(xb[1, u], wi1b[1], preferred_element_type=F32)
            else:
                h1 = jnp.concatenate([h1in[u, j] for j in range(n_col)], axis=1)
                part = jnp.dot(h1, wi2b[...].reshape(512, 2048), preferred_element_type=F32)
            out = zout.at[l, u % 2]
            out[...] = part + bias2[l]

            @pl.when((p == 0) | (p == 3))
            def _():
                arrival(za, za_recv, u).wait_recv()
                out[...] += za[u]

            @pl.when(p == 0)
            def _():
                arrival(zb, zb_recv, u).wait_recv()
                out[...] += zb[u]

            departure(l, u, True)

        def ahead(u, carry):
            input_sum(0, u)
            return carry

        lax.fori_loop(0, AHEAD, ahead, 0)

        def step(t, carry):
            @pl.when(t + AHEAD < steps)
            def _():
                input_sum(0, t + AHEAD)

            remote(h1in.at[t], h1in.at[t], h1_send.at[0], h1_recv.at[t], at(xx, 1 - cc)).wait_recv()
            input_sum(1, t)
            return carry

        lax.fori_loop(0, steps, step, 0)
        for l in range(2):
            for u in range(steps - 2, steps):
                departure(l, u, False)

    for l in range(2):
        @pl.when(jnp.logical_not(is_rec & (layer == l)))
        def _(l=l):
            small_copies(l, False)
            weight_copies(l, False)

    @pl.when(jnp.logical_not(is_input))
    def _():
        for cp in to_input:
            cp.wait_send()

    @pl.when(jnp.logical_not(is_rec & (layer == 0)))
    def _():
        remote(c1_out, c1_out, c_send.at[0], c_recv.at[0], at(xx, 1 - cc)).wait_recv()

    @pl.when(jnp.logical_not(is_rec & (layer == 1)))
    def _():
        remote(c2_out, c2_out, c_send.at[0], c_recv.at[1], at(xx, 1 - cc)).wait_recv()
        for n in range(n_out):
            rows = pl.ds(n * OUT_STEPS, OUT_STEPS)
            remote(h2_out.at[rows], h2_out.at[rows], o_send.at[0], o_recv.at[n], at(xx, 1 - cc)).wait_recv()


def solution(mesh):
    n_row, n_col = mesh.shape["row"], mesh.shape["col"]

    def gate_major(w, unit):
        rows = w.shape[0]
        w = w.reshape(rows, n_row // 4, 4, 4, unit).transpose(0, 1, 3, 2, 4)
        return w.reshape(rows, n_row * 4 * unit)

    def local_program(seq_in, w_in1, w_rec1, b_gate1, w_in2, w_rec2, b_gate2, h_init, c_init):
        steps, batch, k_rows = seq_in.shape
        unit = b_gate1.shape[0] // 4
        cols = w_in1.shape[1]
        col, row = lax.axis_index("col"), lax.axis_index("row")

        def by_owner(w):
            return gate_major(w, unit).reshape(n_col, unit, cols)

        bias = jnp.stack([b_gate1, b_gate2]).reshape(2, 1, 4, 1, unit)
        bias = lax.dynamic_update_slice(
            jnp.zeros((2, n_row // 4, 4, 4, unit), F32), bias, (0, row // 4, 0, row % 4, 0)).reshape(2, 1, cols)
        c_own = lax.dynamic_slice_in_dim(c_init, col * unit, unit, axis=2)
        c_pad = lax.dynamic_update_slice(jnp.zeros((2, batch, 2 * unit), F32), c_own, (0, 0, (row % 2) * unit))
        hid = n_row * unit

        hbm = pl.BlockSpec(memory_space=pl.ANY)
        dma = pltpu.SemaphoreType.DMA
        vm = pltpu.VMEM
        h2_pair, c1_pair, c2_pair = pl.pallas_call(
            functools.partial(lstm_kernel, n_row, n_col),
            out_shape=(
                jax.ShapeDtypeStruct((steps, batch, 2 * unit), BF16),
                jax.ShapeDtypeStruct((batch, 2 * unit), F32),
                jax.ShapeDtypeStruct((batch, 2 * unit), F32),
            ),
            in_specs=[hbm] * 8,
            out_specs=(hbm, hbm, hbm),
            scratch_shapes=[
                vm((n_col, n_row, unit, cols), BF16),
                vm((2, k_rows, cols), BF16),
                vm((n_col, 2, unit, cols), BF16),
                vm((2, steps, batch, k_rows), BF16),
                vm((2, 2, 1, cols), F32),
                vm((2, 1, cols), F32),
                vm((steps + 1, n_col, 2, batch, hid // 2), BF16),
                vm((steps, batch, cols), F32),
                vm((steps, batch, cols), F32),
                vm((steps, n_col, batch, 2 * unit), BF16),
                vm((2, 2, batch, cols), F32),
                vm((batch, cols), F32),
                vm((2, batch, hid // 2), F32),
                vm((n_row, batch, k_rows), BF16),
                vm((n_row, batch, 2 * unit), F32),
                dma((2,)), dma((n_row,)), dma((n_col,)), dma((n_col,)), dma((n_col,)),
                dma((4,)), dma((4,)), dma((4,)),
                dma((2, 2)), dma((n_row,)), dma((n_row,)),
                dma((2, n_col - 1, 2)), dma((2, n_col, 2)),
                dma((steps,)), dma((steps,)), dma((2, 2)),
                dma((n_row // 2,)), dma((steps,)),
                dma((n_row,)), dma((steps // OUT_STEPS,)),
                dma((n_row,)), dma((2,)),
            ],
            compiler_params=pltpu.CompilerParams(
                collective_id=0, has_side_effects=True, vmem_limit_bytes=60 * 2**20),
        )(
            by_owner(w_rec1), by_owner(w_rec2), gate_major(w_in1, unit), by_owner(w_in2),
            seq_in, bias, h_init.astype(BF16), c_pad,
        )

        def own_half(pair):
            return lax.dynamic_slice_in_dim(pair, (row % 2) * unit, unit, axis=pair.ndim - 1)

        return own_half(h2_pair), own_half(c1_pair), own_half(c2_pair)

    row_spec = P(None, "dp", "row")
    weight_spec = P("row", "col")
    bias_spec = P(("col", "row"))
    seq_out_spec = P(None, "dp", ("row", "col"))
    cell_out_spec = P("dp", ("row", "col"))
    return jax.shard_map(
        local_program,
        mesh=mesh,
        in_specs=(row_spec, weight_spec, weight_spec, bias_spec, weight_spec, weight_spec, bias_spec, row_spec, row_spec),
        out_specs=(seq_out_spec, cell_out_spec, cell_out_spec),
        check_vma=False,
    )
```

time: 5540 us -> 1040 us (0.19)
  waiting for transfers between devices: 3790 us -> 0 us
  blocking collectives: 1230 us -> 0 us
  Pallas kernels: 0 us -> 1010 us
  matrix products: 317 us -> 0 us
  other arithmetic: 142 us -> 0.61 us
    reduce_scatter x128 -> x0, waiting for transfers between devices: 3780 us -> none  [lstm_step(): lax.psum_scatter(part_sum, 'row', scatter_dimension=1, tiled=True) + b_own]
    all_gather x128 -> x0, blocking collectives: 1230 us -> none  [lstm_step(): h_next = lax.all_gather(h_own, 'col', axis=1, tiled=True)]
    pallas_call x0 -> x1, Pallas kernels: none -> 1010 us  [local_program(): pl.pallas_call(functools.partial(lstm_kernel, n_row, n_col), out_shape=(j...]
    dot_general x256 -> x0, matrix products: 317 us -> none  [the longest x128 200 us: lstm_step(): part_sum = jnp.dot(in_step, w_in, preferred_element_type=jnp.float32)]
    add x128 -> x0, other arithmetic: 92.2 us -> none  [lstm_step(): lax.psum_scatter(part_sum, 'row', scatter_dimension=1, tiled=True) + b_own]
  transfers between devices with their start and end apart: 128 -> 0, of which waited for: 128 -> 0; matrix products, arithmetic and copies ran while one was open for 0% -> 0% of each run, Pallas kernels for 0% -> 0%
where the time goes in v1:
time: 1040 us
  Pallas kernels  1010 us (97%)
  local copies, waits for them, and re-layouts  25.6 us (2%)
    pallas_call x1, Pallas kernels, local_program(): pl.pallas_call(functools.partial(lstm_kernel, n_row, n_col), out_shape=(j...  1010 us

profile of v1, /device:TPU:97, one launch (start us, length us, event | category | flops | bytes accessed | tf_op | source)
XLA Modules:
  0.0 1041.2 jit_solution(5226107507113075300)
XLA Ops:
  0.6 0.0 copy-start
  0.7 0.8 stack.10
  1.4 0.8 stack.9
  2.3 0.7 reshape.34.bias
  3.0 0.1 constant_dynamic-slice_fusion.3
  3.0 0.4 dynamic_update_slice.7.c0
  3.4 1.5 copy.18
  4.9 2.0 copy.19
  6.9 2.4 reshape_reshape.10.wr2
  9.3 1.5 copy.22
  10.8 2.0 copy.23
  12.8 2.4 reshape_reshape.11.wi2
  15.2 1.5 copy.16
  16.7 2.0 copy.17
  18.7 0.0 copy-start.1
  18.7 2.4 reshape_reshape.9.wr1
  21.1 0.5 copy.20
  21.6 0.0 copy-start.3
  21.7 0.1 copy.21
  21.8 1.4 copy.24.wi1
  23.2 0.6 convert_element_type.3.h0
  23.8 1014.2 %shard_map.112 = (bf16[64,16,128]{2,1,0:T(8,128)(2,1)}, f32[16,128]{1,0:T(8,128)}, f32[16,128]{1,0:T(8,128)}) custom-call(bf16[4,64,2048]{2,1,0:T(8,128)(2,1)} %reshape_reshape.9.wr1, bf16[4,64,2048]{2,1,0:T(8,128)(2,1)} %reshape_reshape.10.wr2, bf16[256,2048]{1,0:T(8,128)(2,1)} %copy.24.wi1, bf16[4,64,2048]{2,1,0:T(8,128)(2,1)} %reshape_reshape.11.wi2, ...), custom_call_target="tpu_custom_call" | custom-call | tf_op jit(solution)/shard_map/pallas_call | solution.py:425
  1038.0 1.4 constant_dynamic-slice_fusion
  1039.4 1.8 constant_dynamic-slice_fusion.2
  (9 shorter events, 0.1 us)
Async XLA Ops:
  0.6 2.3 copy-start
  3.4 3.5 copy-start.2
  18.7 2.4 copy-start.1
  21.6 1.6 copy-start.3

commit v2 on v1

--- a/solution.py
+++ b/solution.py
@@ -9,7 +9,8 @@
 
 MESH = pl.DeviceIdType.MESH
 F32, BF16 = jnp.float32, jnp.bfloat16
-AHEAD = 4
+AHEAD = (3, 6, 10, 6)
+FIRST = (3, 4, 10, 4)
 OUT_STEPS = 8
 
 
@@ -356,13 +357,19 @@
             input_sum(0, u)
             return carry
 
-        lax.fori_loop(0, AHEAD, ahead, 0)
+        def by_place(values):
+            p = place[0]
+            return jnp.where(p == 0, values[0], jnp.where(p == 1, values[1], jnp.where(p == 2, values[2], values[3])))
+
+        first, lead = by_place(FIRST), by_place(AHEAD)
+
+        def made(t):
+            return jnp.minimum(steps, jnp.minimum(first + 2 * t, lead + t))
+
+        lax.fori_loop(0, first, ahead, 0)
 
         def step(t, carry):
-            @pl.when(t + AHEAD < steps)
-            def _():
-                input_sum(0, t + AHEAD)
-
+            lax.fori_loop(made(t), made(t + 1), ahead, 0)
             remote(h1in.at[t], h1in.at[t], h1_send.at[0], h1_recv.at[t], at(xx, 1 - cc)).wait_recv()
             input_sum(1, t)
             return carry

time: 1040 us -> 351 us (0.34)
  Pallas kernels: 1010 us -> 323 us
    pallas_call x1, Pallas kernels: 1010 us -> 323 us  [local_program(): pl.pallas_call(functools.partial(lstm_kernel, n_row, n_col), out_shape=(j...]
where the time goes in v2:
time: 351 us; the launch traced here: 350 us
  Pallas kernels  323 us (92%)
  local copies, waits for them, and re-layouts  25.6 us (7%)
    pallas_call x1, Pallas kernels, local_program(): pl.pallas_call(functools.partial(lstm_kernel, n_row, n_col), out_shape=(j...  323 us
    another operation x3, local copies, waits for them, and re-layouts, by_owner(): return gate_major(w, unit).reshape(n_col, unit, cols)  7.28 us

profile of v2, /device:TPU:97, one launch (start us, length us, event | category | flops | bytes accessed | tf_op | source)
XLA Modules:
  0.0 350.3 jit_solution(14783853378489434124)
XLA Ops:
  0.6 0.0 copy-start
  0.7 0.8 stack.10
  1.4 0.8 stack.9
  2.3 0.7 reshape.34.bias
  3.0 0.1 constant_dynamic-slice_fusion.3
  3.0 0.4 dynamic_update_slice.7.c0
  3.4 1.5 copy.18
  4.9 2.0 copy.19
  6.9 2.4 reshape_reshape.10.wr2
  9.3 1.5 copy.22
  10.8 2.0 copy.23
  12.8 2.4 reshape_reshape.11.wi2
  15.2 1.5 copy.16
  16.7 2.0 copy.17
  18.7 0.0 copy-start.1
  18.7 2.4 reshape_reshape.9.wr1
  21.1 0.5 copy.20
  21.6 0.0 copy-start.3
  21.7 0.1 copy.21
  21.8 1.4 copy.24.wi1
  23.2 0.6 convert_element_type.3.h0
  23.8 323.3 %shard_map.112 = (bf16[64,16,128]{2,1,0:T(8,128)(2,1)}, f32[16,128]{1,0:T(8,128)}, f32[16,128]{1,0:T(8,128)}) custom-call(bf16[4,64,2048]{2,1,0:T(8,128)(2,1)} %reshape_reshape.9.wr1, bf16[4,64,2048]{2,1,0:T(8,128)(2,1)} %reshape_reshape.10.wr2, bf16[256,2048]{1,0:T(8,128)(2,1)} %copy.24.wi1, bf16[4,64,2048]{2,1,0:T(8,128)(2,1)} %reshape_reshape.11.wi2, ...), custom_call_target="tpu_custom_call" | custom-call | tf_op jit(solution)/shard_map/pallas_call | solution.py:432
  347.1 1.4 constant_dynamic-slice_fusion
  348.5 1.8 constant_dynamic-slice_fusion.2
  (9 shorter events, 0.1 us)
Async XLA Ops:
  0.6 2.3 copy-start
  3.4 3.5 copy-start.2
  18.7 2.4 copy-start.1
  21.6 1.6 copy-start.3

commit v3 on v0

v3 whole, which is shorter than its diff:
```python
import functools

import jax
import jax.numpy as jnp
from jax import lax
from jax.experimental import pallas as pl
from jax.experimental.pallas import tpu as pltpu
from jax.sharding import PartitionSpec as P


MESH = pl.DeviceIdType.MESH
F32, BF16 = jnp.float32, jnp.bfloat16
AHEAD = (6, 9, 13, 12)
FIRST = (4, 4, 13, 4)
EARLY = 4
MIDDLE = (3, 2)
H1_AHEAD = 3
OUT_STEPS = 2


def sigmoid(v):
    return 0.5 * jnp.tanh(0.5 * v) + 0.5


def lstm_kernel(
    n_row, n_col, wr1, wr2, wi1, wi2, x_in, b1, b2, h0, c0, h2_out, c1_out, c2_out,
    raw, perm, relay, wbuf, wi1b, wi2b, xb, bb, bias2, hist, za, zb, zc, zmid, h1in, zout, zpre, cst, hin, cin, hst, cstart, bst,
    raw_sem, w_send, w_recv, rel_recv, rel_send, in_send, in_recv, x_local, hc_send, hin_recv, cin_recv,
    hx_send, hx_recv, za_recv, zb_recv, zc_recv, z_send, zm_send, h1_send, h1_recv, o_send, o_recv, c_send, c_recv, passed,
):
    steps = x_in.shape[0]
    n_x = n_row // 2
    col, row = lax.axis_index("col"), lax.axis_index("row")
    xx, cc = row // 2, row % 2
    in_block = (xx < 2) == (col < 2)
    layer = xx // 2
    is_rec = in_block & (cc == 1)
    is_input = in_block == (cc == 0)
    not_input = jnp.logical_not(is_input)

    def at(x, c, y):
        return {"row": x * 2 + c, "col": y}

    def input_core(x, y):
        return jnp.where((x < 2) == (y < 2), 0, 1)

    def owner_at(l, k):
        away = (k + n_col - 2 * l) % n_col // 2
        return at(2 * l + away, 1, jnp.where(away == 0, k, n_col - 1 - k))

    def remote(src, dst, ssem, rsem, dev):
        return pltpu.make_async_remote_copy(
            src_ref=src, dst_ref=dst, send_sem=ssem, recv_sem=rsem, device_id=dev, device_id_type=MESH)

    me_else = at(xx, 1 - cc, col)

    loads = [pltpu.make_async_copy(w, raw.at[i], raw_sem.at[i]) for i, w in enumerate((wr1, wr2, wi1, wi2))]
    for load in loads:
        load.start()
    barrier = pltpu.get_barrier_semaphore()
    for dy in range(n_col):
        for dx in range(n_row):
            if dx or dy:
                pl.semaphore_signal(
                    barrier, inc=1, device_id={"row": (row + dx) % n_row, "col": (col + dy) % n_col}, device_id_type=MESH)

    lane_half = lax.broadcasted_iota(jnp.int32, (1, 128), 1) // 64

    def gate_major(i):
        for q in range(n_row // 2):
            for pair in range(2):
                left = raw[i, :, q * 512 + pair * 128:q * 512 + pair * 128 + 128]
                right = raw[i, :, q * 512 + 256 + pair * 128:q * 512 + 256 + pair * 128 + 128]
                to = (q // 2) * 1024 + pair * 512 + (q % 2) * 128
                low = jnp.concatenate([left[:, :64], right[:, :64]], axis=1)
                high = jnp.concatenate([left[:, 64:], right[:, 64:]], axis=1)
                perm[i, :, :, to:to + 128] = low.reshape(4, 64, 128)
                perm[i, :, :, to + 256:to + 384] = high.reshape(4, 64, 128)

    def to_half(tile, odd):
        moved = jnp.where(odd == row % 2, tile, pltpu.roll(tile, 64, 1))
        return jnp.where(lane_half == row % 2, moved, 0.0)

    for l in range(2):
        hst[l] = h0[l].astype(BF16)
        cells = jnp.where(col < 2, c0[l, :, :128], c0[l, :, 128:])
        cstart[l] = to_half(cells, col % 2)
        for m in range(4):
            gate = to_half((b1, b2)[l][:, (m // 2) * 128:(m // 2) * 128 + 128], m % 2)
            for half in range(2):
                for part in range(2):
                    cols = half * 1024 + m * 256 + part * 128
                    mine = (row // 4 == half) & (row % 4 // 2 == part)
                    bst[l, :, cols:cols + 128] = jnp.where(mine, gate, 0.0)
    for i in range(2):
        loads[i].wait()
        gate_major(i)
    pl.semaphore_wait(barrier, n_row * n_col - 1)

    def start_up(l, go):
        xr, kr = (xx + n_x - 2 * l) % n_x, (col + n_col - 2 * l) % n_col
        home = kr < 2
        other_row = n_col - 1 - col
        mine = home & (xr == 0) & (cc == 1)
        by_near = home & (xr == 2) & (cc == 0)
        by_far = jnp.logical_not(home) & (xr == 2)
        by_corner = jnp.logical_not(home) & ((xr == 3) | ((xr == 0) & (cc == 0)))
        relayed = by_near | by_far | by_corner
        rx = jnp.where(by_near, (2 * l + 1) % n_x, jnp.where(by_far, (2 * l + 2) % n_x, 2 * l))
        rdev = at(rx, jnp.where(by_far, 0, 1), jnp.where(by_near, col, other_row))
        slot = jnp.where(by_near, 0, jnp.where(by_far, cc, jnp.where(xr == 0, 0, 2 - cc)))
        owner = owner_at(l, col)
        small = [
            remote(hst.at[l], hin.at[row], hc_send.at[l, 0], hin_recv.at[row], owner),
            remote(cstart.at[l], cin.at[row], hc_send.at[l, 1], cin_recv.at[row], owner),
        ]
        direct = [remote(perm.at[l, j], wbuf.at[j, row], w_send.at[l, j], w_recv.at[row, j], owner) for j in range(n_col)]
        by_relay = [remote(perm.at[l, j], relay.at[slot, j], w_send.at[l, j], rel_recv.at[slot, j], rdev) for j in range(n_col)]

        @pl.when(jnp.logical_not(mine))
        def _():
            for cp in small:
                cp.start() if go else cp.wait_send()

        @pl.when(jnp.logical_not(mine | relayed))
        def _():
            for cp in direct:
                cp.start() if go else cp.wait_send()

        @pl.when(relayed)
        def _():
            for cp in by_relay:
                cp.start() if go else cp.wait_send()

        if go:
            @pl.when(mine)
            def _():
                wbuf[:, row] = perm[l]
                hin[row] = hst[l]
                cin[row] = cstart[l]

    for l in range(2):
        start_up(l, True)

    x_load = pltpu.make_async_copy(x_in, xb.at[cc], x_local.at[0])
    give = [
        remote(s, d, in_send.at[i], in_recv.at[i], me_else) for i, (s, d) in enumerate((
            (x_in, xb.at[cc]), (bst, bb.at[cc]), (perm.at[2], wi1b.at[cc]), (perm.at[3], wi2b.at[:, cc])))
    ]

    @pl.when(is_input)
    def _():
        x_load.start()
        bb[cc] = bst[...]

    @pl.when(not_input)
    def _():
        give[0].start()
        give[1].start()

    for i in (2, 3):
        loads[i].wait()
        gate_major(i)

        @pl.when(is_input)
        def _(i=i):
            if i == 2:
                wi1b[cc] = perm[2]
            else:
                wi2b[:, cc] = perm[3]

        @pl.when(not_input)
        def _(i=i):
            give[i].start()

    def pass_on(l, slots, sources, to_x):
        dev = at(to_x, 1, col)
        for group in slots:
            for j in range(n_col):
                for s in group:
                    remote(relay.at[s, j], relay.at[s, j], rel_send.at[s, j], rel_recv.at[s, j], dev).wait_recv()
                    remote(relay.at[s, j], wbuf.at[j, sources[s]], rel_send.at[s, j], w_recv.at[sources[s], j], dev).start()
        for group in slots:
            for j in range(n_col):
                for s in group:
                    remote(relay.at[s, j], wbuf.at[j, sources[s]], rel_send.at[s, j], w_recv.at[sources[s], j], dev).wait_send()

    for l in range(2):
        x0, x1, x2, x3 = [(2 * l + i) % n_x for i in range(4)]
        here = (col // 2) == l

        @pl.when(here & (cc == 1) & (xx == x0))
        def _(l=l, x0=x0, x1=x1, x3=x3):
            pass_on(l, ((1, 2), (0,)), (2 * x0, 2 * x3 + 1, 2 * x3), x1)

        @pl.when(here & (cc == 1) & (xx == x1))
        def _(l=l, x0=x0, x2=x2):
            pass_on(l, ((0,),), (2 * x2,), x0)

        @pl.when(here & (cc == 0) & (xx == x2))
        def _(l=l, x1=x1, x2=x2):
            pass_on(l, ((0, 1),), (2 * x2, 2 * x2 + 1), x1)
            if l == 0:
                pl.semaphore_signal(passed, inc=1, device_id=me_else, device_id_type=MESH)

    @pl.when(is_rec)
    def _():
        home = xx % 2 == 0
        own = jnp.where(home, col, n_col - 1 - col)
        last = (own + 2) % n_col

        def peer(d):
            k = (own + d) % n_col
            away = (k + n_col - 2 * layer) % n_col // 2
            return at(2 * layer + away, 1, jnp.where(away == 0, k, n_col - 1 - k))

        def h_copy(t, owner, d, par):
            ref = hist.at[t, owner]
            return remote(ref, ref, hx_send.at[par, d - 1], hx_recv.at[par, owner], peer(d))

        def product(t, owner, cols=slice(None)):
            w = wbuf[owner, :, :, cols].reshape(512, -1)
            return jnp.dot(hist[t, owner], w, preferred_element_type=F32)

        def z_arrives(t):
            remote(za.at[t], za.at[t], z_send.at[0, 0], za_recv.at[t], me_else).wait_recv()
            zpre[...] += za[t]

            @pl.when(home)
            def _():
                remote(zb.at[t], zb.at[t], z_send.at[0, 0], zb_recv.at[t], me_else).wait_recv()
                remote(zc.at[t], zc.at[t], z_send.at[0, 0], zc_recv.at[t], me_else).wait_recv()
                zpre[...] += zb[t] + zc[t]

        def forward(t, go):
            near = jnp.where(home, 0, 1), jnp.where(home, 3, 2)
            for i, (x, y) in enumerate(((near[1], col), (near[1], n_col - 1 - col), (near[0], n_col - 1 - col), (near[0], col))):
                src = hist.at[t + 1, :, :, pl.ds(pl.multiple_of(x * 128, 128), 128)]
                cp = remote(src, h1in.at[t], h1_send.at[i], h1_recv.at[t], at(x, int(i < 3), y))
                cp.start() if go else cp.wait_send()

        def hand_h1(t):
            return remote(h1in.at[t], h1in.at[t], h1_send.at[0], h1_recv.at[t], me_else)

        def middle(u, go):
            cp = remote(zmid.at[u % 2], zc.at[u], zm_send.at[u % 2], zc_recv.at[u], at(2 * layer, 1, col))
            if not go:
                cp.wait_send()
                return
            remote(zb.at[u], zb.at[u], z_send.at[0, 0], zb_recv.at[u], me_else).wait_recv()
            remote(zc.at[u], zc.at[u], z_send.at[0, 0], zc_recv.at[u], me_else).wait_recv()
            zmid[u % 2] = zb[u] + zc[u]
            cp.start()

        lead = jnp.where(layer == 0, MIDDLE[0], MIDDLE[1])

        def out_copy(src, dst, ssem, rsem, r, home_row, go):
            away = remote(src, dst, ssem, rsem, {"row": r, "col": own})
            if r != home_row:
                away.start() if go else away.wait_send()
                return
            local = pltpu.make_async_copy(src, dst, ssem)

            @pl.when(home)
            def _():
                local.start() if go else local.wait()

            @pl.when(jnp.logical_not(home))
            def _():
                away.start() if go else away.wait_send()

        def out_copies(n):
            rows = pl.ds(n * OUT_STEPS, OUT_STEPS)
            for r in range(n_row):
                src = hist.at[pl.ds(n * OUT_STEPS + 1, OUT_STEPS), own, :, pl.ds((r // 2) * 128, 128)]
                out_copy(src, h2_out.at[rows], o_send.at[r], o_recv.at[0], r, 5, True)

        def outs_sent():
            for r in range(n_row):
                out_copy(h2_out, h2_out, o_send.at[r], o_recv.at[0], r, 5, False)

        def c_copies(l, go):
            for r in range(n_row):
                x = r // 2
                src = cst.at[x // 2, :, pl.ds((x % 2) * 128, 128)]
                out_copy(src, (c1_out, c2_out)[l], c_send.at[r], c_recv.at[l], r, 4 * l + 1, go)

        for r in range(n_row):
            @pl.when(jnp.logical_not(home & (row == r)))
            def _(r=r):
                remote(hst.at[0], hin.at[r], hc_send.at[0, 0], hin_recv.at[r], me_else).wait_recv()
                remote(cstart.at[0], cin.at[r], hc_send.at[0, 1], cin_recv.at[r], me_else).wait_recv()
        for x in range(n_x):
            cst[x // 2, :, (x % 2) * 128:(x % 2) * 128 + 128] = cin[2 * x] + cin[2 * x + 1]
        hist[0, last] = jnp.zeros(hist.shape[2:], BF16)
        for r in range(n_row):
            @pl.when(jnp.logical_not(home & (row == r)))
            def _(r=r):
                for j in range(n_col):
                    remote(perm.at[0, j], wbuf.at[j, r], w_send.at[0, j], w_recv.at[r, j], me_else).wait_recv()

        start = jnp.dot(hin[0], wbuf[:, 0].reshape(256, 2048), preferred_element_type=F32)
        for r in range(1, n_row):
            start += jnp.dot(hin[r], wbuf[:, r].reshape(256, 2048), preferred_element_type=F32)
        zpre[...] = start

        @pl.when(layer == 1)
        def _():
            for u in range(H1_AHEAD):
                hand_h1(u).wait_recv()
                hand_h1(u).start()
                hand_h1(u).wait_send()

        @pl.when(jnp.logical_not(home))
        def _():
            for u in range(max(MIDDLE)):
                @pl.when(u < lead)
                def _(u=u):
                    if u >= 2:
                        middle(u - 2, False)
                    middle(u, True)

        z_arrives(0)

        def finish(t, send):
            par, par_before = t % 2, (t + 1) % 2

            @pl.when(t > 0)
            def _():
                h_copy(t, last, 2, par_before).wait_recv()

            z = []
            for g in range(8):
                cols = slice(g * 256, g * 256 + 256)
                z.append(product(t, last, cols) + zpre[:, cols])
            for half in range(2):
                i, f, g, o = z[half * 4:half * 4 + 4]
                c_new = sigmoid(f) * cst[half] + sigmoid(i) * jnp.tanh(g)
                cst[half] = c_new
                hist[t + 1, own, :, half * 256:half * 256 + 256] = (sigmoid(o) * jnp.tanh(c_new)).astype(BF16)
            if send:
                for d in (2, 1, 3):
                    h_copy(t + 1, own, d, par).start()

        def sent(t):
            for d in (2, 1, 3):
                h_copy(t + 1, own, d, t % 2).wait_send()

        def outputs(t):
            @pl.when((layer == 1) & (t % OUT_STEPS == OUT_STEPS - 1))
            def _():
                out_copies(t // OUT_STEPS)

        def step(t, carry):
            par = t % 2
            finish(t, True)
            zpre[...] = product(t + 1, own)
            u = t + lead

            @pl.when(jnp.logical_not(home) & (u < steps))
            def _():
                middle(u - 2, False)
                middle(u, True)

            @pl.when((layer == 1) & (t + H1_AHEAD < steps))
            def _():
                @pl.when(t > 0)
                def _():
                    hand_h1(t + H1_AHEAD).wait_send()

                hand_h1(t + H1_AHEAD).wait_recv()
                hand_h1(t + H1_AHEAD).start()

            z_arrives(t + 1)

            @pl.when((t > 1) & (layer == 0))
            def _():
                forward(t - 2, False)

            @pl.when((t > 0) & (layer == 0))
            def _():
                forward(t - 1, True)

            @pl.when(t > 0)
            def _():
                sent(t - 1)

            outputs(t)
            owners = [(own + d) % n_col for d in (1, 3)]
            for d, owner in zip((1, 3), owners):
                h_copy(t + 1, owner, d, par).wait_recv()
            zpre[...] += product(t + 1, owners[0]) + product(t + 1, owners[1])

            return carry

        lax.fori_loop(0, steps - 1, step, 0)
        end = steps - 1

        @pl.when(jnp.logical_not(home))
        def _():
            middle(steps - 2, False)
            middle(steps - 1, False)

        sent(end - 1)

        @pl.when(layer == 0)
        def _():
            forward(end - 2, False)
            finish(end, True)
            c_copies(0, True)
            forward(end - 1, True)
            forward(end - 1, False)
            for d in (1, 3, 2):
                h_copy(steps, (own + d) % n_col, d, end % 2).wait_recv()
            forward(end, True)
            forward(end, False)
            sent(end)
            c_copies(0, False)

        @pl.when(layer == 1)
        def _():
            hand_h1(0).wait_send()
            finish(end, False)
            outputs(end)
            c_copies(1, True)
            outs_sent()
            c_copies(1, False)

    @pl.when(is_input)
    def _():
        x_load.wait()
        for i, ref in enumerate((xb.at[1 - cc], bb.at[1 - cc], wi1b.at[1 - cc], wi2b.at[:, 1 - cc])):
            remote(ref, ref, in_send.at[i], in_recv.at[i], me_else).wait_recv()
        bias2[...] = bb[0] + bb[1]

        places, heads, middles, homes = [], [], [], []
        for l in range(2):
            xr, kr = (xx + n_x - 2 * l) % n_x, (col + n_col - 2 * l) % n_col
            places.append(jnp.where(kr < 2, xr, (1 + n_x - xr) % n_x))
            heads.append((2 * l + jnp.where(kr < 2, 0, 1)) % n_x)
            homes.append(kr < 2)
            middles.append((2 * l + jnp.where(kr < 2, 1, 0)) % n_x)

        def arrival(buf, sem, u):
            return remote(buf.at[u], buf.at[u], z_send.at[0, 0], sem.at[u], me_else)

        def departure(l, u, start):
            p, home = places[l], homes[l]
            src = zout.at[l, u % 2]
            dst_x = jnp.where(p == 2, middles[l], jnp.where(home & (p == 1), xx, heads[l]))
            on = at(dst_x, jnp.where(home, 1, input_core(dst_x, col)), col)
            owner = owner_at(l, col)
            dev = {axis: jnp.where(p == 0, owner[axis], on[axis]) for axis in ("row", "col")}
            ways = [remote(src, buf.at[u], z_send.at[l, u % 2], sem.at[u], dev)
                    for buf, sem in ((za, za_recv), (zb, zb_recv), (zc, zc_recv))]
            if not start:
                ways[0].wait_send()
                return
            to_c = home & (p == 1)
            to_b = (home & (p >= 2)) | (jnp.logical_not(home) & (p == 1))
            for way, here in zip(ways, (jnp.logical_not(to_b | to_c), to_b, to_c)):
                @pl.when(here)
                def _(way=way):
                    way.start()

        def input_sum(l, u):
            p = places[l]

            @pl.when(u >= 2)
            def _():
                departure(l, u - 2, False)

            if l == 0:
                part = jnp.dot(xb[0, u], wi1b[0].reshape(256, 2048), preferred_element_type=F32)
                part += jnp.dot(xb[1, u], wi1b[1].reshape(256, 2048), preferred_element_type=F32)
            else:
                h1 = jnp.concatenate([h1in[u, j] for j in range(n_col)], axis=1)
                part = jnp.dot(h1, wi2b[...].reshape(512, 2048), preferred_element_type=F32)
            out = zout.at[l, u % 2]
            out[...] = part + bias2[l]
            adds = jnp.logical_not(homes[l])

            @pl.when(adds & (p < 2))
            def _():
                arrival(za, za_recv, u).wait_recv()
                out[...] += za[u]

            @pl.when(adds & (p == 0))
            def _():
                arrival(zb, zb_recv, u).wait_recv()
                out[...] += zb[u]

            departure(l, u, True)

        def ahead(u, carry):
            input_sum(0, u)
            return carry

        def by_place(values):
            p = places[0]
            return jnp.where(p == 0, values[0], jnp.where(p == 1, values[1], jnp.where(p == 2, values[2], values[3])))

        first, lead = by_place(FIRST), by_place(AHEAD)

        def made(t):
            return jnp.minimum(steps, jnp.minimum(first + 2 * t, lead + t))

        early = jnp.minimum(made(0), EARLY)
        lax.fori_loop(0, early, ahead, 0)

        @pl.when((places[0] == 2) & (col < 2))
        def _():
            pl.semaphore_wait(passed, 1)

        lax.fori_loop(early, made(0), ahead, 0)

        def step(t, carry):
            lax.fori_loop(made(t), made(t + 1), ahead, 0)
            remote(h1in.at[t], h1in.at[t], h1_send.at[0], h1_recv.at[t], me_else).wait_recv()
            input_sum(1, t)
            return carry

        lax.fori_loop(0, steps, step, 0)
        for l in range(2):
            for u in range(steps - 2, steps):
                departure(l, u, False)

    for l in range(2):
        start_up(l, False)

    @pl.when(not_input)
    def _():
        for cp in give:
            cp.wait_send()

    keeps_own = is_rec & (xx % 2 == 0)
    for l, out in enumerate((c1_out, c2_out)):
        @pl.when(jnp.logical_not(keeps_own & (layer == l)))
        def _(l=l, out=out):
            remote(out, out, c_send.at[0], c_recv.at[l], me_else).wait_recv()

    @pl.when(jnp.logical_not(keeps_own & (layer == 1)))
    def _():
        remote(h2_out, h2_out, o_send.at[0], o_recv.at[0], me_else).wait_recv()


def solution(mesh):
    n_row, n_col = mesh.shape["row"], mesh.shape["col"]

    def local_program(seq_in, w_in1, w_rec1, b_gate1, w_in2, w_rec2, b_gate2, h_init, c_init):
        steps, batch, k_rows = seq_in.shape
        unit = b_gate1.shape[0] // 4
        cols = w_in1.shape[1]
        row = lax.axis_index("row")
        hid = n_row * unit

        hbm = pl.BlockSpec(memory_space=pl.ANY)
        near = pl.BlockSpec(memory_space=pltpu.VMEM)
        dma = pltpu.SemaphoreType.DMA
        vm = pltpu.VMEM
        h2_pair, c1_pair, c2_pair = pl.pallas_call(
            functools.partial(lstm_kernel, n_row, n_col),
            out_shape=(
                jax.ShapeDtypeStruct((steps, batch, 2 * unit), BF16),
                jax.ShapeDtypeStruct((batch, 2 * unit), F32),
                jax.ShapeDtypeStruct((batch, 2 * unit), F32),
            ),
            in_specs=[hbm] * 5 + [near] * 4,
            out_specs=(hbm, hbm, hbm),
            scratch_shapes=[
                vm((4, k_rows, cols), BF16),
                vm((4, n_col, unit, cols), BF16),
                vm((3, n_col, unit, cols), BF16),
                vm((n_col, n_row, unit, cols), BF16),
                vm((2, n_col, unit, cols), BF16),
                vm((n_col, 2, unit, cols), BF16),
                vm((2, steps, batch, k_rows), BF16),
                vm((2, 2, 1, cols), F32),
                vm((2, 1, cols), F32),
                vm((steps + 1, n_col, batch, hid), BF16),
                vm((steps, batch, cols), F32),
                vm((steps, batch, cols), F32),
                vm((steps, batch, cols), F32),
                vm((2, batch, cols), F32),
                vm((steps, n_col, batch, 2 * unit), BF16),
                vm((2, 2, batch, cols), F32),
                vm((batch, cols), F32),
                vm((2, batch, hid // 2), F32),
                vm((n_row, batch, k_rows), BF16),
                vm((n_row, batch, 2 * unit), F32),
                vm((2, batch, k_rows), BF16),
                vm((2, batch, 2 * unit), F32),
                vm((2, 1, cols), F32),
                dma((4,)), dma((2, n_col)), dma((n_row, n_col)), dma((3, n_col)), dma((3, n_col)),
                dma((4,)), dma((4,)), dma((1,)),
                dma((2, 2)), dma((n_row,)), dma((n_row,)),
                dma((2, n_col - 1)), dma((2, n_col)),
                dma((steps,)), dma((steps,)), dma((steps,)), dma((2, 2)), dma((2,)),
                dma((n_row // 2,)), dma((steps,)),
                dma((n_row,)), dma((1,)),
                dma((n_row,)), dma((2,)), pltpu.SemaphoreType.REGULAR,
            ],
            compiler_params=pltpu.CompilerParams(
                collective_id=0, has_side_effects=True, vmem_limit_bytes=60 * 2**20),
        )(
            w_rec1, w_rec2, w_in1, w_in2, seq_in, b_gate1.reshape(1, -1), b_gate2.reshape(1, -1), h_init, c_init,
        )

        def own_half(pair):
            return lax.dynamic_slice_in_dim(pair, (row % 2) * unit, unit, axis=pair.ndim - 1)

        return own_half(h2_pair), own_half(c1_pair), own_half(c2_pair)

    row_spec = P(None, "dp", "row")
    weight_spec = P("row", "col")
    bias_spec = P(("col", "row"))
    seq_out_spec = P(None, "dp", ("row", "col"))
    cell_out_spec = P("dp", ("row", "col"))
    return jax.shard_map(
        local_program,
        mesh=mesh,
        in_specs=(row_spec, weight_spec, weight_spec, bias_spec, weight_spec, weight_spec, bias_spec, row_spec, row_spec),
        out_specs=(seq_out_spec, cell_out_spec, cell_out_spec),
        check_vma=False,
    )
```

time: 5540 us -> 294 us (0.05)
  waiting for transfers between devices: 3790 us -> 0 us
  blocking collectives: 1230 us -> 0 us
  matrix products: 317 us -> 0 us
  Pallas kernels: 0 us -> 291 us
  other arithmetic: 142 us -> 0 us
    reduce_scatter x128 -> x0, waiting for transfers between devices: 3780 us -> none  [lstm_step(): lax.psum_scatter(part_sum, 'row', scatter_dimension=1, tiled=True) + b_own]
    all_gather x128 -> x0, blocking collectives: 1230 us -> none  [lstm_step(): h_next = lax.all_gather(h_own, 'col', axis=1, tiled=True)]
    dot_general x256 -> x0, matrix products: 317 us -> none  [the longest x128 200 us: lstm_step(): part_sum = jnp.dot(in_step, w_in, preferred_element_type=jnp.float32)]
    pallas_call x0 -> x1, Pallas kernels: none -> 291 us  [local_program(): pl.pallas_call(functools.partial(lstm_kernel, n_row, n_col), out_shape=(j...]
    add x128 -> x0, other arithmetic: 92.2 us -> none  [lstm_step(): lax.psum_scatter(part_sum, 'row', scatter_dimension=1, tiled=True) + b_own]
  transfers between devices with their start and end apart: 128 -> 0, of which waited for: 128 -> 0; matrix products, arithmetic and copies ran while one was open for 0% -> 0% of each run, Pallas kernels for 0% -> 0%
where the time goes in v3:
time: 294 us
  Pallas kernels  291 us (99%)
    pallas_call x1, Pallas kernels, local_program(): pl.pallas_call(functools.partial(lstm_kernel, n_row, n_col), out_shape=(j...  291 us

profile of v3, /device:TPU:97, one launch (start us, length us, event | category | flops | bytes accessed | tf_op | source)
XLA Modules:
  0.0 293.7 jit_solution(115401318803450824)
XLA Ops:
  0.6 290.6 %shard_map.112 = (bf16[64,16,128]{2,1,0:T(8,128)(2,1)}, f32[16,128]{1,0:T(8,128)}, f32[16,128]{1,0:T(8,128)}) custom-call(bf16[256,2048]{1,0:T(8,128)(2,1)} %wr1.1, bf16[256,2048]{1,0:T(8,128)(2,1)} %wr2.1, bf16[256,2048]{1,0:T(8,128)(2,1)} %wi1.1, bf16[256,2048]{1,0:T(8,128)(2,1)} %wi2.1, bf16[64,16,256]{2,1,0:T(8,128)(2,1)} %x_in.1, f32[1,256]{1,0:T(1,128)} %bitcast.2, ...), custom_call_target="tpu_custom_call" | custom-call | tf_op jit(solution)/shard_map/pallas_call | solution.py:561
  291.2 0.0 copy-start
  291.2 0.0 copy-start.1
  291.2 1.8 constant_dynamic-slice_fusion.2
  293.1 0.0 copy-done
  293.1 0.0 copy-done.1
  293.1 0.7 constant_dynamic-slice_fusion
Async XLA Ops:
  291.2 1.8 copy-start
  291.2 1.8 copy-start.1

commit v4 on v3

--- a/solution.py
+++ b/solution.py
@@ -53,6 +53,13 @@
             src_ref=src, dst_ref=dst, send_sem=ssem, recv_sem=rsem, device_id=dev, device_id_type=MESH)
 
     me_else = at(xx, 1 - cc, col)
+
+    def dots(pieces):
+        sums = [jnp.dot(rows, weights, preferred_element_type=F32) for rows, weights in pieces]
+        return functools.reduce(jnp.add, sums)
+
+    def cols_of(tile):
+        return slice(tile * 256, tile * 256 + 256)
 
     loads = [pltpu.make_async_copy(w, raw.at[i], raw_sem.at[i]) for i, w in enumerate((wr1, wr2, wi1, wi2))]
     for load in loads:
@@ -214,13 +221,13 @@
             away = (k + n_col - 2 * layer) % n_col // 2
             return at(2 * layer + away, 1, jnp.where(away == 0, k, n_col - 1 - k))
 
-        def h_copy(t, owner, d, par):
-            ref = hist.at[t, owner]
-            return remote(ref, ref, hx_send.at[par, d - 1], hx_recv.at[par, owner], peer(d))
-
-        def product(t, owner, cols=slice(None)):
-            w = wbuf[owner, :, :, cols].reshape(512, -1)
-            return jnp.dot(hist[t, owner], w, preferred_element_type=F32)
+        def h_copy(t, owner, half, d, par):
+            ref = hist.at[t, owner, half]
+            return remote(ref, ref, hx_send.at[par, d - 1, half], hx_recv.at[par, owner, half], peer(d))
+
+        def products(t, pieces, cols=slice(None)):
+            return dots([
+                (hist[t, owner, half], wbuf[owner, half * 4:half * 4 + 4, :, cols].reshape(256, -1)) for owner, half in pieces])
 
         def z_arrives(t):
             remote(za.at[t], za.at[t], z_send.at[0, 0], za_recv.at[t], me_else).wait_recv()
@@ -235,7 +242,7 @@
         def forward(t, go):
             near = jnp.where(home, 0, 1), jnp.where(home, 3, 2)
             for i, (x, y) in enumerate(((near[1], col), (near[1], n_col - 1 - col), (near[0], n_col - 1 - col), (near[0], col))):
-                src = hist.at[t + 1, :, :, pl.ds(pl.multiple_of(x * 128, 128), 128)]
+                src = hist.at[t + 1, :, x // 2, :, pl.ds(pl.multiple_of(x % 2 * 128, 128), 128)]
                 cp = remote(src, h1in.at[t], h1_send.at[i], h1_recv.at[t], at(x, int(i < 3), y))
                 cp.start() if go else cp.wait_send()
 
@@ -272,7 +279,7 @@
         def out_copies(n):
             rows = pl.ds(n * OUT_STEPS, OUT_STEPS)
             for r in range(n_row):
-                src = hist.at[pl.ds(n * OUT_STEPS + 1, OUT_STEPS), own, :, pl.ds((r // 2) * 128, 128)]
+                src = hist.at[pl.ds(n * OUT_STEPS + 1, OUT_STEPS), own, r // 4, :, pl.ds(r // 2 % 2 * 128, 128)]
                 out_copy(src, h2_out.at[rows], o_send.at[r], o_recv.at[0], r, 5, True)
 
         def outs_sent():
@@ -299,11 +306,6 @@
                 for j in range(n_col):
                     remote(perm.at[0, j], wbuf.at[j, r], w_send.at[0, j], w_recv.at[r, j], me_else).wait_recv()
 
-        start = jnp.dot(hin[0], wbuf[:, 0].reshape(256, 2048), preferred_element_type=F32)
-        for r in range(1, n_row):
-            start += jnp.dot(hin[r], wbuf[:, r].reshape(256, 2048), preferred_element_type=F32)
-        zpre[...] = start
-
         @pl.when(layer == 1)
         def _():
             for u in range(H1_AHEAD):
@@ -320,6 +322,7 @@
                         middle(u - 2, False)
                     middle(u, True)
 
+        zpre[...] = dots([(hin[r], wbuf[:, r].reshape(256, -1)) for r in range(n_row)])
         z_arrives(0)
 
         def finish(t, send):
@@ -327,24 +330,23 @@
 
             @pl.when(t > 0)
             def _():
-                h_copy(t, last, 2, par_before).wait_recv()
-
-            z = []
-            for g in range(8):
-                cols = slice(g * 256, g * 256 + 256)
-                z.append(product(t, last, cols) + zpre[:, cols])
+                h_copy(t, last, 0, 2, par_before).wait_recv()
+                h_copy(t, last, 1, 2, par_before).wait_recv()
+
+            z = [products(t, ((last, 0), (last, 1)), cols_of(tile)) + zpre[:, cols_of(tile)] for tile in range(8)]
             for half in range(2):
                 i, f, g, o = z[half * 4:half * 4 + 4]
                 c_new = sigmoid(f) * cst[half] + sigmoid(i) * jnp.tanh(g)
                 cst[half] = c_new
-                hist[t + 1, own, :, half * 256:half * 256 + 256] = (sigmoid(o) * jnp.tanh(c_new)).astype(BF16)
-            if send:
-                for d in (2, 1, 3):
-                    h_copy(t + 1, own, d, par).start()
+                hist[t + 1, own, half] = (sigmoid(o) * jnp.tanh(c_new)).astype(BF16)
+                if send:
+                    for d in (1, 3, 2):
+                        h_copy(t + 1, own, half, d, par).start()
 
         def sent(t):
-            for d in (2, 1, 3):
-                h_copy(t + 1, own, d, t % 2).wait_send()
+            for half in range(2):
+                for d in (1, 3, 2):
+                    h_copy(t + 1, own, half, d, t % 2).wait_send()
 
         def outputs(t):
             @pl.when((layer == 1) & (t % OUT_STEPS == OUT_STEPS - 1))
@@ -354,7 +356,8 @@
         def step(t, carry):
             par = t % 2
             finish(t, True)
-            zpre[...] = product(t + 1, own)
+            beside, across = (own + 1) % n_col, (own + 3) % n_col
+            zpre[...] = products(t + 1, ((own, 0), (own, 1)))
             u = t + lead
 
             @pl.when(jnp.logical_not(home) & (u < steps))
@@ -386,10 +389,10 @@
                 sent(t - 1)
 
             outputs(t)
-            owners = [(own + d) % n_col for d in (1, 3)]
-            for d, owner in zip((1, 3), owners):
-                h_copy(t + 1, owner, d, par).wait_recv()
-            zpre[...] += product(t + 1, owners[0]) + product(t + 1, owners[1])
+            for half in range(2):
+                h_copy(t + 1, beside, half, 1, par).wait_recv()
+                h_copy(t + 1, across, half, 3, par).wait_recv()
+                zpre[...] += products(t + 1, ((beside, half), (across, half)))
 
             return carry
 
@@ -411,7 +414,8 @@
             forward(end - 1, True)
             forward(end - 1, False)
             for d in (1, 3, 2):
-                h_copy(steps, (own + d) % n_col, d, end % 2).wait_recv()
+                for half in range(2):
+                    h_copy(steps, (own + d) % n_col, half, d, end % 2).wait_recv()
             forward(end, True)
             forward(end, False)
             sent(end)
@@ -471,13 +475,13 @@
                 departure(l, u - 2, False)
 
             if l == 0:
-                part = jnp.dot(xb[0, u], wi1b[0].reshape(256, 2048), preferred_element_type=F32)
-                part += jnp.dot(xb[1, u], wi1b[1].reshape(256, 2048), preferred_element_type=F32)
+                part = dots([(xb[i, u], wi1b[i].reshape(256, -1)) for i in range(2)])
             else:
                 h1 = jnp.concatenate([h1in[u, j] for j in range(n_col)], axis=1)
-                part = jnp.dot(h1, wi2b[...].reshape(512, 2048), preferred_element_type=F32)
+                part = dots([(h1, wi2b[...].reshape(512, -1))])
             out = zout.at[l, u % 2]
             out[...] = part + bias2[l]
+
             adds = jnp.logical_not(homes[l])
 
             @pl.when(adds & (p < 2))
@@ -577,7 +581,7 @@
                 vm((2, steps, batch, k_rows), BF16),
                 vm((2, 2, 1, cols), F32),
                 vm((2, 1, cols), F32),
-                vm((steps + 1, n_col, batch, hid), BF16),
+                vm((steps + 1, n_col, 2, batch, hid // 2), BF16),
                 vm((steps, batch, cols), F32),
                 vm((steps, batch, cols), F32),
                 vm((steps, batch, cols), F32),
@@ -594,7 +598,7 @@
                 dma((4,)), dma((2, n_col)), dma((n_row, n_col)), dma((3, n_col)), dma((3, n_col)),
                 dma((4,)), dma((4,)), dma((1,)),
                 dma((2, 2)), dma((n_row,)), dma((n_row,)),
-                dma((2, n_col - 1)), dma((2, n_col)),
+                dma((2, n_col - 1, 2)), dma((2, n_col, 2)),
                 dma((steps,)), dma((steps,)), dma((steps,)), dma((2, 2)), dma((2,)),
                 dma((n_row // 2,)), dma((steps,)),
                 dma((n_row,)), dma((1,)),

time: 294 us -> 276 us (0.939)
  Pallas kernels: 291 us -> 272 us
    pallas_call x1, Pallas kernels: 291 us -> 272 us  [local_program(): pl.pallas_call(functools.partial(lstm_kernel, n_row, n_col), out_shape=(j...]
where the time goes in v4:
time: 276 us; the launch traced here: 275 us
  Pallas kernels  272 us (99%)
    pallas_call x1, Pallas kernels, local_program(): pl.pallas_call(functools.partial(lstm_kernel, n_row, n_col), out_shape=(j...  272 us

profile of v4, /device:TPU:97, one launch (start us, length us, event | category | flops | bytes accessed | tf_op | source)
XLA Modules:
  0.0 275.3 jit_solution(11138472188123815001)
XLA Ops:
  0.6 272.2 %shard_map.112 = (bf16[64,16,128]{2,1,0:T(8,128)(2,1)}, f32[16,128]{1,0:T(8,128)}, f32[16,128]{1,0:T(8,128)}) custom-call(bf16[256,2048]{1,0:T(8,128)(2,1)} %wr1.1, bf16[256,2048]{1,0:T(8,128)(2,1)} %wr2.1, bf16[256,2048]{1,0:T(8,128)(2,1)} %wi1.1, bf16[256,2048]{1,0:T(8,128)(2,1)} %wi2.1, bf16[64,16,256]{2,1,0:T(8,128)(2,1)} %x_in.1, f32[1,256]{1,0:T(1,128)} %bitcast.2, ...), custom_call_target="tpu_custom_call" | custom-call | tf_op jit(solution)/shard_map/pallas_call | solution.py:565
  272.8 0.0 copy-start
  272.9 0.0 copy-start.1
  272.9 1.8 constant_dynamic-slice_fusion.2
  274.7 0.0 copy-done
  274.7 0.0 copy-done.1
  274.7 0.7 constant_dynamic-slice_fusion
Async XLA Ops:
  272.8 1.8 copy-start
  272.9 1.8 copy-start.1

commit v5 on v4

v5 whole, which is shorter than its diff:
```python
import functools

import jax
import jax.numpy as jnp
from jax import lax
from jax.experimental import pallas as pl
from jax.experimental.pallas import tpu as pltpu
from jax.sharding import PartitionSpec as P


MESH = pl.DeviceIdType.MESH
F32, BF16 = jnp.float32, jnp.bfloat16
HALVES = LAYERS = (0, 1)
GATES = 4
LANES, TILE, PAIR, OWN = 128, 256, 512, 1024
HALF_LANES = 64
CHUNK = 32
HELD = 2
AHEAD = (5, 8, 12, 8)
FIRST = (4, 4, 7, 6)
EARLY = 4
MIDDLE = (3, 2)
H1_AHEAD = 3
RING = 32
OUT_STEPS = 2
LATE = 8
PEERS = (1, 3, 2)


def sigmoid(v):
    return 0.5 * jnp.tanh(0.5 * v) + 0.5


def lstm_kernel(
    n_row, n_col, wr1, wr2, wi1, wi2, x_in, b1, b2, h0, c0, h2_out, c1_out, c2_out,
    raw, perm, relay, wbuf, wi1b, wi2b, xb, bb, bias2, init, hist, za, zb, zc, zmid, h1in, zout, zpre, cst, cin, cstart, bst,
    raw_sem, w_send, w_recv, rel_recv, rel_send, in_send, in_recv, x_local, c0_send, cin_recv,
    hx_send, hx_recv, za_recv, zb_recv, zc_recv, z_send, zm_send, h1_send, h1_recv, o_send, o_recv, c_send, c_recv, passed,
):
    steps = x_in.shape[0]
    n_x = n_row // 2
    n_part = raw.shape[1] // CHUNK
    per_col = n_part // n_col
    col, row = lax.axis_index("col"), lax.axis_index("row")
    xx, cc = row // 2, row % 2
    in_block = (xx < 2) == (col < 2)
    layer = xx // 2
    is_rec = in_block & (cc == 1)
    is_input = in_block == (cc == 0)
    not_input = jnp.logical_not(is_input)
    other_row = n_col - 1 - col

    def at(x, c, y):
        return {"row": x * 2 + c, "col": y}

    def input_core(x, y):
        return jnp.where((x < 2) == (y < 2), 0, 1)

    def is_away(l, k):
        return (k + n_col - 2 * l) % n_col // 2

    def owner_at(l, k):
        away = is_away(l, k)
        return at(2 * l + away, 1, jnp.where(away == 0, k, n_col - 1 - k))

    def remote(src, dst, ssem, rsem, dev):
        return pltpu.make_async_remote_copy(
            src_ref=src, dst_ref=dst, send_sem=ssem, recv_sem=rsem, device_id=dev, device_id_type=MESH)

    me_else = at(xx, 1 - cc, col)

    def arrived(ref, sem):
        remote(ref, ref, x_local.at[0], sem, me_else).wait_recv()

    def run(copies, go):
        for cp in copies:
            cp.start() if go else cp.wait_send()

    def dots(pieces):
        sums = [jnp.dot(rows, weights, preferred_element_type=F32) for rows, weights in pieces]
        return functools.reduce(jnp.add, sums)

    def cols_of(tile):
        return slice(tile * TILE, tile * TILE + TILE)

    loads = [pltpu.make_async_copy(w, raw.at[i], raw_sem.at[i]) for i, w in enumerate((wr1, wr2, wi1, wi2))]
    for load in loads:
        load.start()
    barrier = pltpu.get_barrier_semaphore()
    for dy in range(n_col):
        for dx in range(n_row):
            if dx or dy:
                pl.semaphore_signal(
                    barrier, inc=1, device_id={"row": (row + dx) % n_row, "col": (col + dy) % n_col}, device_id_type=MESH)

    lane_half = lax.broadcasted_iota(jnp.int32, (1, LANES), 1) // HALF_LANES

    def gate_major(i):
        for q in range(n_x):
            for pair in HALVES:
                at_left = q * PAIR + pair * LANES
                left, right = raw[i, :, at_left:at_left + LANES], raw[i, :, at_left + TILE:at_left + TILE + LANES]
                to = q // 2 * OWN + pair * PAIR + q % 2 * LANES
                low = jnp.concatenate([left[:, :HALF_LANES], right[:, :HALF_LANES]], axis=1)
                high = jnp.concatenate([left[:, HALF_LANES:], right[:, HALF_LANES:]], axis=1)
                for part, start in ((low, to), (high, to + TILE)):
                    perm[i, :, :, start:start + LANES] = part.reshape(n_col, -1, LANES)

    def to_half(tile, odd):
        moved = jnp.where(odd == row % 2, tile, pltpu.roll(tile, HALF_LANES, 1))
        return jnp.where(lane_half == row % 2, moved, 0.0)

    for l in LAYERS:
        cells = jnp.where(col < 2, c0[l, :, :LANES], c0[l, :, LANES:])
        cstart[l] = to_half(cells, col % 2)
        for m in range(GATES):
            start = m // 2 * LANES
            gate = to_half((b1, b2)[l][:, start:start + LANES], m % 2)
            for half in HALVES:
                for part in HALVES:
                    start = half * OWN + m * TILE + part * LANES
                    mine = (row // 4 == half) & (row % 4 // 2 == part)
                    bst[l, :, start:start + LANES] = jnp.where(mine, gate, 0.0)
    for l in LAYERS:
        loads[l].wait()
        gate_major(l)
    pl.semaphore_wait(barrier, n_row * n_col - 1)

    def part_of(ref, c):
        return ref.at[c // per_col, pl.ds(c % per_col * CHUNK, CHUNK)]

    def start_up(l, go, chunks):
        xr, kr = (xx + n_x - 2 * l) % n_x, (col + n_col - 2 * l) % n_col
        home = kr < 2
        mine = home & (xr == 0) & (cc == 1)
        by_near = home & (xr == 2) & (cc == 0)
        by_far = jnp.logical_not(home) & (xr == 2)
        by_corner = jnp.logical_not(home) & ((xr == 3) | ((xr == 0) & (cc == 0)))
        relayed = by_near | by_far | by_corner
        rx = jnp.where(by_near, (2 * l + 1) % n_x, jnp.where(by_far, (2 * l + 2) % n_x, 2 * l))
        rdev = at(rx, jnp.where(by_far, 0, 1), jnp.where(by_near, col, other_row))
        slot = jnp.where(by_near, 0, jnp.where(by_far, cc, jnp.where(xr == 0, 0, 2 - cc)))
        owner = owner_at(l, col)
        cells = [remote(cstart.at[l], cin.at[row], c0_send.at[l], cin_recv.at[row], owner)]
        direct, by_relay = [], []
        for c in chunks:
            src = part_of(perm.at[l], c)
            direct.append(remote(src, part_of(wbuf.at[:, row], c), w_send.at[l], w_recv.at[row], owner))
            by_relay.append(remote(src, part_of(relay.at[slot], c), w_send.at[l], rel_recv.at[slot, c], rdev))
        if not go:
            direct = by_relay = [remote(perm.at[l], perm.at[l], w_send.at[l], w_recv.at[row], owner)]
        if chunks[0] == 0:
            @pl.when(jnp.logical_not(mine))
            def _():
                run(cells, go)

            if go:
                @pl.when(mine)
                def _():
                    wbuf[:, row] = perm[l]
                    cin[row] = cstart[l]

        @pl.when(jnp.logical_not(mine | relayed))
        def _():
            run(direct, go)

        @pl.when(relayed)
        def _():
            run(by_relay, go)

    all_chunks = range(n_part)
    held = all_chunks[n_part - HELD:]
    for l in LAYERS:
        start_up(l, True, all_chunks[:n_part - HELD])

    @pl.when(not_input)
    def _():
        for l in LAYERS:
            start_up(l, True, held)

    for l in LAYERS:
        init[cc, l] = jnp.dot(h0[l].astype(BF16), perm[l].reshape(-1, perm.shape[-1]), preferred_element_type=F32)
    x_load = pltpu.make_async_copy(x_in, xb.at[cc], x_local.at[0])
    give = [remote(s, d, in_send.at[i], in_recv.at[i], me_else) for i, (s, d) in enumerate((
        (x_in, xb.at[cc]), (bst, bb.at[cc]), (init.at[cc], init.at[cc]), (perm.at[2], wi1b.at[cc]), (perm.at[3], wi2b.at[:, cc])))]
    soon = len(give) - 2

    @pl.when(is_input)
    def _():
        x_load.start()
        bb[cc] = bst[...]

    @pl.when(not_input)
    def _():
        run(give[:soon], True)

    for l in LAYERS:
        loads[2 + l].wait()
        gate_major(2 + l)

        @pl.when(is_input)
        def _(l=l):
            (wi1b.at[cc], wi2b.at[:, cc])[l][...] = perm[2 + l]

        @pl.when(not_input)
        def _(l=l):
            give[soon + l].start()

    def pass_on(slots, sources, to_x):
        dev = at(to_x, 1, col)

        def onward(s, c):
            return remote(part_of(relay.at[s], c), part_of(wbuf.at[:, sources[s]], c), rel_send.at[s],
                          w_recv.at[sources[s]], dev)

        for group in slots:
            for c in all_chunks:
                for s in group:
                    arrived(part_of(relay.at[s], c), rel_recv.at[s, c])
                    onward(s, c).start()

        def done():
            for group in slots:
                for s in group:
                    remote(relay.at[s], relay.at[s], rel_send.at[s], rel_recv.at[s, 0], dev).wait_send()

        return done

    def relays(then):
        for l in LAYERS:
            x0, x1, x2, x3 = [(2 * l + i) % n_x for i in range(n_x)]
            here = (col // 2) == l
            for core, x, args in (
                (1, x0, (((1, 2), (0,)), (2 * x0, 2 * x3 + 1, 2 * x3), x1)),
                (1, x1, (((0,),), (2 * x2,), x0)),
                (0, x2, (((0, 1),), (2 * x2, 2 * x2 + 1), x1)),
            ):
                yield l, core, here & (cc == core) & (xx == x), args

    for l, core, mine, args in relays(None):
        @pl.when(mine)
        def _(l=l, core=core, args=args):
            done = pass_on(*args)
            if core == 0:
                done()
                if l == 0:
                    pl.semaphore_signal(passed.at[0], inc=1, device_id=me_else, device_id_type=MESH)

    @pl.when(is_rec)
    def _():
        home = xx % 2 == 0
        own = jnp.where(home, col, other_row)
        beside, across, last = [(own + d) % n_col for d in PEERS]

        def peer(d):
            k = (own + d) % n_col
            away = is_away(layer, k)
            return at(2 * layer + away, 1, jnp.where(away == 0, k, n_col - 1 - k))

        def h_copy(t, owner, half, d):
            ref = hist.at[t + 1, owner, half]
            return remote(ref, ref, hx_send.at[t % 2, d - 1, half], hx_recv.at[t % 2, owner, half], peer(d))

        def products(t, pieces, cols=slice(None)):
            return dots([(hist[t + 1, owner, half], wbuf[owner, half * GATES:half * GATES + GATES, :, cols].reshape(TILE, -1))
                         for owner, half in pieces])

        def z_arrives(t):
            arrived(za.at[t], za_recv.at[t % RING])
            zpre[...] += za[t]

            @pl.when(home)
            def _():
                arrived(zb.at[t], zb_recv.at[t % RING])
                arrived(zc.at[t], zc_recv.at[t % RING])
                zpre[...] += zb[t] + zc[t]

        def forward(t, go):
            near, far = jnp.where(home, 0, 1), jnp.where(home, 3, 2)
            for i, (x, c, y) in enumerate(((far, 1, col), (far, 1, other_row), (near, 1, other_row), (near, 0, col))):
                src = hist.at[t + 1, :, x // 2, :, pl.ds(pl.multiple_of(x % 2 * LANES, LANES), LANES)]
                run([remote(src, h1in.at[t], h1_send.at[i], h1_recv.at[t % RING], at(x, c, y))], go)

        def hand_h1(t):
            return remote(h1in.at[t], h1in.at[t], h1_send.at[0], h1_recv.at[t % RING], me_else)

        def middle(u, go):
            cp = remote(zmid.at[u % 2], zc.at[u], zm_send.at[u % 2], zc_recv.at[u % RING], at(2 * layer, 1, col))
            if go:
                arrived(zb.at[u], zb_recv.at[u % RING])
                arrived(zc.at[u], zc_recv.at[u % RING])
                zmid[u % 2] = zb[u] + zc[u]
            run([cp], go)

        lead = jnp.where(layer == 0, MIDDLE[0], MIDDLE[1])

        def out_copy(src, dst, ssem, rsem, r, home_row, go):
            away = remote(src, dst, ssem, rsem, {"row": r, "col": own})
            if r != home_row:
                run([away], go)
                return
            local = pltpu.make_async_copy(src, dst, ssem)

            @pl.when(home)
            def _():
                local.start() if go else local.wait()

            @pl.when(jnp.logical_not(home))
            def _():
                run([away], go)

        home_two = n_row // 2 + 1

        def pair_of(ref, r):
            return ref.at[r // 4, :, pl.ds(r // 2 % 2 * LANES, LANES)]

        def out_copies(n):
            rows = pl.ds(n * OUT_STEPS, OUT_STEPS)
            phase = n * OUT_STEPS // (steps - LATE)
            for r in range(n_row):
                src = hist.at[pl.ds(n * OUT_STEPS + 1, OUT_STEPS), own, r // 4, :, pl.ds(r // 2 % 2 * LANES, LANES)]

                def send(r=r, src=src):
                    out_copy(src, h2_out.at[rows], o_send.at[r, phase], o_recv.at[phase], r, home_two, True)

                if r % 2:
                    send()
                else:
                    pl.when((phase == 1) | (home & (r + 1 == home_two)))(send)

        def outs_sent():
            for phase, ref in enumerate((h2_out.at[pl.ds(0, steps - LATE)], h2_out.at[pl.ds(0, LATE)])):
                for r in range(n_row):
                    def sent(r=r, ref=ref, phase=phase):
                        out_copy(ref, ref, o_send.at[r, phase], o_recv.at[phase], r, home_two, False)

                    if r % 2 or phase:
                        sent()
                    elif r + 1 == home_two:
                        pl.when(home)(sent)

        def c_copies(l, go):
            for r in range(n_row):
                out_copy(pair_of(cst, r), (c1_out, c2_out)[l], c_send.at[r], c_recv.at[l], r, n_x * l + 1, go)

        for r in range(n_row):
            @pl.when(jnp.logical_not(home & (row == r)))
            def _(r=r):
                arrived(cin.at[r], cin_recv.at[r])
        for x in range(n_x):
            pair_of(cst, 2 * x)[...] = cin[2 * x] + cin[2 * x + 1]

        for u in range(H1_AHEAD):
            @pl.when(layer == 1)
            def _(u=u):
                hand = hand_h1(u)
                hand.wait_recv()
                hand.start()
                hand.wait_send()

            @pl.when(jnp.logical_not(home) & (u < lead))
            def _(u=u):
                if u >= 2:
                    middle(u - 2, False)
                middle(u, True)

        zpre[...] = jnp.zeros_like(zpre)
        z_arrives(0)

        def gates(t, z, send):
            for half in HALVES:
                i, f, g, o = z[half * GATES:half * GATES + GATES]
                c_new = sigmoid(f) * cst[half] + sigmoid(i) * jnp.tanh(g)
                cst[half] = c_new
                hist[t + 1, own, half] = (sigmoid(o) * jnp.tanh(c_new)).astype(BF16)
                if send:
                    run([h_copy(t, own, half, d) for d in PEERS], True)

        tiles = range(2 * GATES)

        def finish(t, send):
            for half in HALVES:
                h_copy(t - 1, last, half, 2).wait_recv()
            pieces = [(last, half) for half in HALVES]
            gates(t, [products(t - 1, pieces, cols_of(tile)) + zpre[:, cols_of(tile)] for tile in tiles], send)

        def sent(t):
            for half in HALVES:
                run([h_copy(t, own, half, d) for d in PEERS], False)

        def outputs(t):
            @pl.when((layer == 1) & (t % OUT_STEPS == OUT_STEPS - 1))
            def _():
                out_copies(t // OUT_STEPS)

        def prepare(t):
            @pl.when((t > 1) & (layer == 0))
            def _():
                forward(t - 2, False)

            @pl.when((t > 0) & (layer == 0))
            def _():
                forward(t - 1, True)

            zpre[...] = products(t, [(own, half) for half in HALVES])
            u = t + lead

            @pl.when(jnp.logical_not(home) & (u < steps))
            def _():
                middle(u - 2, False)
                middle(u, True)

            @pl.when((layer == 1) & (t + H1_AHEAD < steps))
            def _():
                hand = hand_h1(t + H1_AHEAD)

                @pl.when(t > 0)
                def _():
                    hand.wait_send()

                hand.wait_recv()
                hand.start()

            @pl.when(t > 0)
            def _():
                sent(t - 1)

            outputs(t)
            for half in HALVES:
                for d, owner in zip(PEERS, (beside, across)):
                    h_copy(t, owner, half, d).wait_recv()
                zpre[...] += products(t, ((beside, half), (across, half)))
                if half == 0:
                    z_arrives(t + 1)

        gates(0, [zpre[:, cols_of(tile)] for tile in tiles], True)
        for _, core, mine, args in relays(None):
            if core == 1:
                @pl.when(mine)
                def _(args=args):
                    slots, sources, to_x = args
                    for group in slots:
                        for s in group:
                            remote(relay.at[s], relay.at[s], rel_send.at[s], rel_recv.at[s, 0], me_else).wait_send()
        for r in range(n_row):
            @pl.when(jnp.logical_not(home & (row == r)))
            def _(r=r):
                arrived(wbuf.at[:, r], w_recv.at[r])

        prepare(0)

        def step(t, carry):
            finish(t, True)
            prepare(t)
            return carry

        lax.fori_loop(1, steps - 1, step, 0)
        end = steps - 1

        @pl.when(jnp.logical_not(home))
        def _():
            middle(end - 1, False)
            middle(end, False)

        sent(end - 1)

        @pl.when(layer == 0)
        def _():
            forward(end - 2, False)
            finish(end, True)
            c_copies(0, True)
            forward(end - 1, True)
            forward(end - 1, False)
            for d, owner in zip(PEERS, (beside, across, last)):
                for half in HALVES:
                    h_copy(end, owner, half, d).wait_recv()
            forward(end, True)
            forward(end, False)
            sent(end)
            c_copies(0, False)

        @pl.when(layer == 1)
        def _():
            hand_h1(0).wait_send()
            finish(end, False)
            outputs(end)
            c_copies(1, True)
            outs_sent()
            c_copies(1, False)

    @pl.when(is_input)
    def _():
        x_load.wait()
        mate = 1 - cc
        for i, ref in enumerate((xb.at[mate], bb.at[mate], init.at[mate], wi1b.at[mate], wi2b.at[:, mate])):
            arrived(ref, in_recv.at[i])
        bias2[...] = bb[0] + bb[1]

        places, heads, middles, homes = [], [], [], []
        for l in LAYERS:
            xr, kr = (xx + n_x - 2 * l) % n_x, (col + n_col - 2 * l) % n_col
            homes.append(kr < 2)
            places.append(jnp.where(kr < 2, xr, (1 + n_x - xr) % n_x))
            heads.append((2 * l + jnp.where(kr < 2, 0, 1)) % n_x)
            middles.append((2 * l + jnp.where(kr < 2, 1, 0)) % n_x)

        def departure(l, u, start):
            p, home = places[l], homes[l]
            src = zout.at[l, u % 2]
            dst_x = jnp.where(p == 2, middles[l], jnp.where(home & (p == 1), xx, heads[l]))
            on = at(dst_x, jnp.where(home, 1, input_core(dst_x, col)), col)
            owner = owner_at(l, col)
            dev = {axis: jnp.where(p == 0, owner[axis], on[axis]) for axis in on}
            ways = [remote(src, buf.at[u], z_send.at[l, u % 2], sem.at[u % RING], dev)
                    for buf, sem in ((za, za_recv), (zb, zb_recv), (zc, zc_recv))]
            if not start:
                ways[0].wait_send()
                return
            to_c = home & (p == 1)
            to_b = (home & (p >= 2)) | (jnp.logical_not(home) & (p == 1))
            for way, here in zip(ways, (jnp.logical_not(to_b | to_c), to_b, to_c)):
                pl.when(here)(way.start)

        def input_sum(l, u):
            p = places[l]

            @pl.when(u >= 2)
            def _():
                departure(l, u - 2, False)

            if l == 0:
                part = dots([(xb[i, u], wi1b[i].reshape(TILE, -1)) for i in HALVES])
            else:
                h1 = jnp.concatenate([h1in[u, j] for j in range(n_col)], axis=1)
                part = dots([(h1, wi2b[...].reshape(2 * TILE, -1))])
            out = zout.at[l, u % 2]
            out[...] = part + bias2[l]

            @pl.when(u == 0)
            def _():
                out[...] += init[0, l] + init[1, l]

            adds = jnp.logical_not(homes[l])

            @pl.when(adds & (p < 2))
            def _():
                arrived(za.at[u], za_recv.at[u % RING])
                out[...] += za[u]

            @pl.when(adds & (p == 0))
            def _():
                arrived(zb.at[u], zb_recv.at[u % RING])
                out[...] += zb[u]

            departure(l, u, True)

        def ahead(u, carry):
            input_sum(0, u)
            return carry

        def by_place(values):
            return functools.reduce(lambda rest, i: jnp.where(places[0] == i, values[i], rest), range(1, n_x), values[0])

        first, lead = by_place(FIRST), by_place(AHEAD)

        def made(t):
            return jnp.minimum(steps, jnp.minimum(first + 2 * t, lead + t))

        soon_made = made(1)
        early = jnp.minimum(soon_made, EARLY)
        lax.fori_loop(0, 1, ahead, 0)
        for l in LAYERS:
            start_up(l, True, held)
        lax.fori_loop(1, early, ahead, 0)

        @pl.when((places[0] == 2) & (col < 2))
        def _():
            pl.semaphore_wait(passed.at[0], 1)

        lax.fori_loop(early, soon_made, ahead, 0)

        def step(t, carry):
            arrived(h1in.at[t], h1_recv.at[t % RING])
            input_sum(1, t)
            lax.fori_loop(made(t + 1), made(t + 2), ahead, 0)
            return carry

        lax.fori_loop(0, steps, step, 0)
        for l in LAYERS:
            for u in HALVES:
                departure(l, steps - 2 + u, False)

    for l in LAYERS:
        start_up(l, False, all_chunks)

    @pl.when(not_input)
    def _():
        run(give, False)

    keeps_own = is_rec & (xx % 2 == 0)
    gets_h2 = jnp.logical_not(keeps_own & (layer == 1))
    early, late = h2_out.at[pl.ds(0, steps - LATE)], h2_out.at[pl.ds(0, LATE)]
    hand_on = remote(early, early, o_send.at[0, 0], o_recv.at[0], me_else)

    @pl.when(gets_h2)
    def _():
        hand_on.wait_recv()
        pl.when(cc == 1)(hand_on.start)

    for l, out in enumerate((c1_out, c2_out)):
        @pl.when(jnp.logical_not(keeps_own & (layer == l)))
        def _(l=l, out=out):
            arrived(out, c_recv.at[l])

    @pl.when(gets_h2)
    def _():
        arrived(late, o_recv.at[1])
        pl.when(cc == 1)(hand_on.wait_send)


def solution(mesh):
    n_row, n_col = mesh.shape["row"], mesh.shape["col"]

    def local_program(seq_in, w_in1, w_rec1, b_gate1, w_in2, w_rec2, b_gate2, h_init, c_init):
        steps, batch, k_rows = seq_in.shape
        unit = b_gate1.shape[0] // GATES
        cols = w_in1.shape[1]
        row = lax.axis_index("row")
        half_own = n_row // 2 * unit
        n_part = k_rows // CHUNK
        pair = 2 * unit

        hbm = pl.BlockSpec(memory_space=pl.ANY)
        near = pl.BlockSpec(memory_space=pltpu.VMEM)
        dma = pltpu.SemaphoreType.DMA
        vm = pltpu.VMEM
        block = (n_col, unit, cols)
        z_all = vm((steps, batch, cols), F32)
        by_step = dma((RING,))
        h2_pair, c1_pair, c2_pair = pl.pallas_call(
            functools.partial(lstm_kernel, n_row, n_col),
            out_shape=(
                jax.ShapeDtypeStruct((steps, batch, pair), BF16),
                jax.ShapeDtypeStruct((batch, pair), F32),
                jax.ShapeDtypeStruct((batch, pair), F32),
            ),
            in_specs=[hbm] * 5 + [near] * 4,
            out_specs=(hbm, hbm, hbm),
            scratch_shapes=[
                vm((4, k_rows, cols), BF16),
                vm((4, *block), BF16),
                vm((3, *block), BF16),
                vm((n_col, n_row, unit, cols), BF16),
                vm((2, *block), BF16),
                vm((n_col, 2, unit, cols), BF16),
                vm((2, steps, batch, k_rows), BF16),
                vm((2, 2, 1, cols), F32),
                vm((2, 1, cols), F32),
                vm((2, 2, batch, cols), F32),
                vm((steps + 1, n_col, 2, batch, half_own), BF16),
                z_all, z_all, z_all,
                vm((2, batch, cols), F32),
                vm((steps, n_col, batch, pair), BF16),
                vm((2, 2, batch, cols), F32),
                vm((batch, cols), F32),
                vm((2, batch, half_own), F32),
                vm((n_row, batch, pair), F32),
                vm((2, batch, pair), F32),
                vm((2, 1, cols), F32),
                dma((4,)), dma((2,)), dma((n_row,)), dma((3, n_part)), dma((3,)),
                dma((5,)), dma((5,)), dma((1,)),
                dma((2,)), dma((n_row,)),
                dma((2, n_col - 1, 2)), dma((2, n_col, 2)),
                by_step, by_step, by_step, dma((2, 2)), dma((2,)),
                dma((n_col,)), by_step,
                dma((n_row, 2)), dma((2,)),
                dma((n_row,)), dma((2,)), pltpu.SemaphoreType.REGULAR((1,)),
            ],
            compiler_params=pltpu.CompilerParams(collective_id=0, has_side_effects=True, vmem_limit_bytes=60 * 2**20),
        )(
            w_rec1, w_rec2, w_in1, w_in2, seq_in, b_gate1.reshape(1, -1), b_gate2.reshape(1, -1), h_init, c_init,
        )

        def own_half(both):
            return lax.dynamic_slice_in_dim(both, (row % 2) * unit, unit, axis=both.ndim - 1)

        return own_half(h2_pair), own_half(c1_pair), own_half(c2_pair)

    row_spec = P(None, "dp", "row")
    weight_spec = P("row", "col")
    bias_spec = P(("col", "row"))
    seq_out_spec = P(None, "dp", ("row", "col"))
    cell_out_spec = P("dp", ("row", "col"))
    return jax.shard_map(
        local_program,
        mesh=mesh,
        in_specs=(row_spec, weight_spec, weight_spec, bias_spec, weight_spec, weight_spec, bias_spec, row_spec, row_spec),
        out_specs=(seq_out_spec, cell_out_spec, cell_out_spec),
        check_vma=False,
    )
```

time: 276 us -> 258 us (0.935)
  Pallas kernels: 272 us -> 254 us
    pallas_call x1, Pallas kernels: 272 us -> 254 us  [local_program(): pl.pallas_call(functools.partial(lstm_kernel, n_row, n_col), out_shape=(j...]
where the time goes in v5:
time: 258 us; the launch traced here: 257 us
  Pallas kernels  254 us (98%)
    pallas_call x1, Pallas kernels, local_program(): pl.pallas_call(functools.partial(lstm_kernel, n_row, n_col), out_shape=(j...  254 us

profile of v5, /device:TPU:97, one launch (start us, length us, event | category | flops | bytes accessed | tf_op | source)
XLA Modules:
  0.0 257.4 jit_solution(12251647254552116734)
XLA Ops:
  0.6 254.2 %shard_map.112 = (bf16[64,16,128]{2,1,0:T(8,128)(2,1)}, f32[16,128]{1,0:T(8,128)}, f32[16,128]{1,0:T(8,128)}) custom-call(bf16[256,2048]{1,0:T(8,128)(2,1)} %wr1.1, bf16[256,2048]{1,0:T(8,128)(2,1)} %wr2.1, bf16[256,2048]{1,0:T(8,128)(2,1)} %wi1.1, bf16[256,2048]{1,0:T(8,128)(2,1)} %wi2.1, bf16[64,16,256]{2,1,0:T(8,128)(2,1)} %x_in.1, f32[1,256]{1,0:T(1,128)} %bitcast.2, ...), custom_call_target="tpu_custom_call" | custom-call | tf_op jit(solution)/shard_map/pallas_call | solution.py:640
  254.8 0.0 copy-start
  254.9 0.0 copy-start.1
  254.9 1.8 constant_dynamic-slice_fusion.2
  256.7 0.0 copy-done
  256.7 0.0 copy-done.1
  256.7 0.7 constant_dynamic-slice_fusion
Async XLA Ops:
  254.8 1.8 copy-start
  254.9 1.8 copy-start.1

commit v6 on v5

--- a/solution.py
+++ b/solution.py
@@ -18,13 +18,14 @@
 HELD = 2
 AHEAD = (5, 8, 12, 8)
 FIRST = (4, 4, 7, 6)
-EARLY = 4
+EARLY = 3
 MIDDLE = (3, 2)
 H1_AHEAD = 3
 RING = 32
 OUT_STEPS = 2
 LATE = 8
 PEERS = (1, 3, 2)
+ORDER = (PEERS, (2, 1, 3))
 
 
 def sigmoid(v):
@@ -121,9 +122,8 @@
                     start = half * OWN + m * TILE + part * LANES
                     mine = (row // 4 == half) & (row % 4 // 2 == part)
                     bst[l, :, start:start + LANES] = jnp.where(mine, gate, 0.0)
-    for l in LAYERS:
-        loads[l].wait()
-        gate_major(l)
+    loads[0].wait()
+    gate_major(0)
     pl.semaphore_wait(barrier, n_row * n_col - 1)
 
     def part_of(ref, c):
@@ -171,11 +171,13 @@
     all_chunks = range(n_part)
     held = all_chunks[n_part - HELD:]
     for l in LAYERS:
+        if l:
+            loads[l].wait()
+            gate_major(l)
         start_up(l, True, all_chunks[:n_part - HELD])
 
-    @pl.when(not_input)
-    def _():
-        for l in LAYERS:
+        @pl.when(not_input)
+        def _(l=l):
             start_up(l, True, held)
 
     for l in LAYERS:
@@ -267,13 +269,14 @@
 
         def z_arrives(t):
             arrived(za.at[t], za_recv.at[t % RING])
-            zpre[...] += za[t]
 
             @pl.when(home)
             def _():
                 arrived(zb.at[t], zb_recv.at[t % RING])
                 arrived(zc.at[t], zc_recv.at[t % RING])
-                zpre[...] += zb[t] + zc[t]
+
+        def input_sums(t):
+            return za[t] + jnp.where(home, zb[t] + zc[t], 0.0)
 
         def forward(t, go):
             near, far = jnp.where(home, 0, 1), jnp.where(home, 3, 2)
@@ -350,22 +353,24 @@
         for x in range(n_x):
             pair_of(cst, 2 * x)[...] = cin[2 * x] + cin[2 * x + 1]
 
-        for u in range(H1_AHEAD):
+        def run_ahead(u):
             @pl.when(layer == 1)
-            def _(u=u):
+            def _():
                 hand = hand_h1(u)
                 hand.wait_recv()
                 hand.start()
                 hand.wait_send()
 
             @pl.when(jnp.logical_not(home) & (u < lead))
-            def _(u=u):
+            def _():
                 if u >= 2:
                     middle(u - 2, False)
                 middle(u, True)
 
-        zpre[...] = jnp.zeros_like(zpre)
+        for u in range(H1_AHEAD):
+            run_ahead(u)
         z_arrives(0)
+        zpre[...] = input_sums(0)
 
         def gates(t, z, send):
             for half in HALVES:
@@ -374,15 +379,16 @@
                 cst[half] = c_new
                 hist[t + 1, own, half] = (sigmoid(o) * jnp.tanh(c_new)).astype(BF16)
                 if send:
-                    run([h_copy(t, own, half, d) for d in PEERS], True)
+                    run([h_copy(t, own, half, d) for d in ORDER[half]], True)
 
         tiles = range(2 * GATES)
 
-        def finish(t, send):
+        def finish(t, send, others):
             for half in HALVES:
                 h_copy(t - 1, last, half, 2).wait_recv()
             pieces = [(last, half) for half in HALVES]
-            gates(t, [products(t - 1, pieces, cols_of(tile)) + zpre[:, cols_of(tile)] for tile in tiles], send)
+            gates(t, [part + products(t - 1, pieces, cols_of(tile)) + zpre[:, cols_of(tile)]
+                      for tile, part in zip(tiles, others)], send)
 
         def sent(t):
             for half in HALVES:
@@ -426,12 +432,16 @@
                 sent(t - 1)
 
             outputs(t)
+            parts = []
             for half in HALVES:
+                if half:
+                    z_arrives(t + 1)
                 for d, owner in zip(PEERS, (beside, across)):
                     h_copy(t, owner, half, d).wait_recv()
-                zpre[...] += products(t, ((beside, half), (across, half)))
-                if half == 0:
-                    z_arrives(t + 1)
+                if half:
+                    zpre[...] += input_sums(t + 1)
+                parts.append([products(t, ((beside, half), (across, half)), cols_of(tile)) for tile in tiles])
+            return [a + b for a, b in zip(*parts)]
 
         gates(0, [zpre[:, cols_of(tile)] for tile in tiles], True)
         for _, core, mine, args in relays(None):
@@ -447,15 +457,14 @@
             def _(r=r):
                 arrived(wbuf.at[:, r], w_recv.at[r])
 
-        prepare(0)
+        end = steps - 1
 
         def step(t, carry):
-            finish(t, True)
-            prepare(t)
+            finish(t + 1, True, prepare(t))
             return carry
 
-        lax.fori_loop(1, steps - 1, step, 0)
-        end = steps - 1
+        lax.fori_loop(0, end - 1, step, 0)
+        others = prepare(end - 1)
 
         @pl.when(jnp.logical_not(home))
         def _():
@@ -467,7 +476,7 @@
         @pl.when(layer == 0)
         def _():
             forward(end - 2, False)
-            finish(end, True)
+            finish(end, True, others)
             c_copies(0, True)
             forward(end - 1, True)
             forward(end - 1, False)
@@ -482,7 +491,7 @@
         @pl.when(layer == 1)
         def _():
             hand_h1(0).wait_send()
-            finish(end, False)
+            finish(end, False, others)
             outputs(end)
             c_copies(1, True)
             outs_sent()

time: 258 us -> 252 us (0.977)
  Pallas kernels: 254 us -> 249 us
    pallas_call x1, Pallas kernels: 254 us -> 249 us  [local_program(): pl.pallas_call(functools.partial(lstm_kernel, n_row, n_col), out_shape=(j...]
where the time goes in v6:
time: 252 us
  Pallas kernels  249 us (99%)
    pallas_call x1, Pallas kernels, local_program(): pl.pallas_call(functools.partial(lstm_kernel, n_row, n_col), out_shape=(j...  249 us

profile of v6, /device:TPU:97, one launch (start us, length us, event | category | flops | bytes accessed | tf_op | source)
XLA Modules:
  0.0 252.0 jit_solution(18397072637566166472)
XLA Ops:
  0.6 248.9 %shard_map.112 = (bf16[64,16,128]{2,1,0:T(8,128)(2,1)}, f32[16,128]{1,0:T(8,128)}, f32[16,128]{1,0:T(8,128)}) custom-call(bf16[256,2048]{1,0:T(8,128)(2,1)} %wr1.1, bf16[256,2048]{1,0:T(8,128)(2,1)} %wr2.1, bf16[256,2048]{1,0:T(8,128)(2,1)} %wi1.1, bf16[256,2048]{1,0:T(8,128)(2,1)} %wi2.1, bf16[64,16,256]{2,1,0:T(8,128)(2,1)} %x_in.1, f32[1,256]{1,0:T(1,128)} %bitcast.2, ...), custom_call_target="tpu_custom_call" | custom-call | tf_op jit(solution)/shard_map/pallas_call | solution.py:649
  249.5 0.0 copy-start
  249.5 0.0 copy-start.1
  249.5 1.8 constant_dynamic-slice_fusion.2
  251.3 0.0 copy-done
  251.3 0.0 copy-done.1
  251.3 0.7 constant_dynamic-slice_fusion
Async XLA Ops:
  249.5 1.8 copy-start
  249.5 1.8 copy-start.1

commit v7 on v6

--- a/solution.py
+++ b/solution.py
@@ -15,13 +15,13 @@
 LANES, TILE, PAIR, OWN = 128, 256, 512, 1024
 HALF_LANES = 64
 CHUNK = 32
-HELD = 2
+HELD = 1
 AHEAD = (5, 8, 12, 8)
 FIRST = (4, 4, 7, 6)
 EARLY = 3
 MIDDLE = (3, 2)
 H1_AHEAD = 3
-RING = 32
+RING = 24
 OUT_STEPS = 2
 LATE = 8
 PEERS = (1, 3, 2)

time: 252 us -> 251 us (level)
  no operation moved by 1% of the time
where the time goes in v7:
time: 251 us
  Pallas kernels  248 us (99%)
    pallas_call x1, Pallas kernels, local_program(): pl.pallas_call(functools.partial(lstm_kernel, n_row, n_col), out_shape=(j...  248 us

profile of v7, /device:TPU:97, one launch (start us, length us, event | category | flops | bytes accessed | tf_op | source)
XLA Modules:
  0.0 251.3 jit_solution(7564503644619005761)
XLA Ops:
  0.6 248.1 %shard_map.112 = (bf16[64,16,128]{2,1,0:T(8,128)(2,1)}, f32[16,128]{1,0:T(8,128)}, f32[16,128]{1,0:T(8,128)}) custom-call(bf16[256,2048]{1,0:T(8,128)(2,1)} %wr1.1, bf16[256,2048]{1,0:T(8,128)(2,1)} %wr2.1, bf16[256,2048]{1,0:T(8,128)(2,1)} %wi1.1, bf16[256,2048]{1,0:T(8,128)(2,1)} %wi2.1, bf16[64,16,256]{2,1,0:T(8,128)(2,1)} %x_in.1, f32[1,256]{1,0:T(1,128)} %bitcast.2, ...), custom_call_target="tpu_custom_call" | custom-call | tf_op jit(solution)/shard_map/pallas_call | solution.py:649
  248.8 0.0 copy-start
  248.8 0.0 copy-start.1
  248.8 1.8 constant_dynamic-slice_fusion.2
  250.6 0.0 copy-done
  250.6 0.0 copy-done.1
  250.6 0.7 constant_dynamic-slice_fusion
Async XLA Ops:
  248.8 1.8 copy-start
  248.8 1.8 copy-start.1

commit v8 on v7

--- a/solution.py
+++ b/solution.py
@@ -384,11 +384,11 @@
         tiles = range(2 * GATES)
 
         def finish(t, send, others):
+            parts = others
             for half in HALVES:
                 h_copy(t - 1, last, half, 2).wait_recv()
-            pieces = [(last, half) for half in HALVES]
-            gates(t, [part + products(t - 1, pieces, cols_of(tile)) + zpre[:, cols_of(tile)]
-                      for tile, part in zip(tiles, others)], send)
+                parts = [part + products(t - 1, ((last, half),), cols_of(tile)) for tile, part in zip(tiles, parts)]
+            gates(t, [part + zpre[:, cols_of(tile)] for tile, part in zip(tiles, parts)], send)
 
         def sent(t):
             for half in HALVES:

time: 251 us -> 249 us (level)
  no operation moved by 1% of the time
where the time goes in v8:
time: 249 us
  Pallas kernels  246 us (99%)
  local copies, waits for them, and re-layouts  2.49 us (1%)
    pallas_call x1, Pallas kernels, local_program(): pl.pallas_call(functools.partial(lstm_kernel, n_row, n_col), out_shape=(j...  246 us

profile of v8, /device:TPU:97, one launch (start us, length us, event | category | flops | bytes accessed | tf_op | source)
XLA Modules:
  0.0 248.8 jit_solution(8519832744102279797)
XLA Ops:
  0.6 245.7 %shard_map.112 = (bf16[64,16,128]{2,1,0:T(8,128)(2,1)}, f32[16,128]{1,0:T(8,128)}, f32[16,128]{1,0:T(8,128)}) custom-call(bf16[256,2048]{1,0:T(8,128)(2,1)} %wr1.1, bf16[256,2048]{1,0:T(8,128)(2,1)} %wr2.1, bf16[256,2048]{1,0:T(8,128)(2,1)} %wi1.1, bf16[256,2048]{1,0:T(8,128)(2,1)} %wi2.1, bf16[64,16,256]{2,1,0:T(8,128)(2,1)} %x_in.1, f32[1,256]{1,0:T(1,128)} %bitcast.2, ...), custom_call_target="tpu_custom_call" | custom-call | tf_op jit(solution)/shard_map/pallas_call | solution.py:649
  246.3 0.0 copy-start
  246.4 0.0 copy-start.1
  246.4 1.8 constant_dynamic-slice_fusion.2
  248.2 0.0 copy-done
  248.2 0.0 copy-done.1
  248.2 0.7 constant_dynamic-slice_fusion
Async XLA Ops:
  246.3 1.8 copy-start
  246.4 1.8 copy-start.1
